TPU v7x, 768 devices: a whole 4x8x12 slice. The times are simulated.
768 devices in a mesh: grp: 96 (over z, y), lane: 8 (over x, core).
Axes of the slice: x: 4, y: 8, z: 12, core: 2. Of those that a mesh axis runs over, the one named last changes fastest.
Arguments:
- grad_pooled: bfloat16 [98304, 32, 256], P(('grp', 'lane')), may hold values from -16 to 16
- bag_len: int32 [98304, 32], P(('grp', 'lane')), may hold values from 1 to 8
- lookup_slot: int32 [98304, 32, 8], P('grp', 'lane'), may hold values from -1 to 191, as said below
- slot_row: int32 [96, 8, 96, 2], P('grp', 'lane'), may hold values from 0 to 1023, as said below
- weights: float32 [32, 24576, 256], P('lane', 'grp'), may hold values from -6 to 6
- accum: float32 [32, 24576], P('lane', 'grp'), may hold values from 0.05 to 0.5
Outputs:
- new_weights: float32 [32, 24576, 256], P('lane', 'grp')
- new_accum: float32 [32, 24576], P('lane', 'grp')
Inputs may be any that keep to these rules, and one draw needn't show every extreme that they name: `lookup_slot`: position j of bag (b, t) holds -1 when j >= bag_len[b, t] and otherwise a slot number s; the row slot_row[s // 2, t // 4, g, s % 2], with g the group of sample b, lies in local table t % 4. `slot_row`: several slots, also from different groups, may name the same row.
All inputs are finite; a program needn't handle non-finite values.
Results may differ from a plain program's by a relative error of at most 0.0035.
Values may be sent and summed in bfloat16 or wider, within the bound.
No kernel may reach another device: no remote copies, remote signals or barrier semaphores. Data moves between devices by JAX's collectives and lax.ppermute only.
A program may use at most 32 MiB of HBM per device.

v0:
```python
import math

import jax
import jax.numpy as jnp
from jax import lax
from jax.sharding import Mesh
from jax.sharding import PartitionSpec as P

SLOTS_PEER = 2
LANE = ("lane_0", "lane_1")
GRP = ("grp_0", "grp_1")
GRP_LANE = ("grp_0", "grp_1", "lane_0", "lane_1")


LEARN_RATE = 0.3
EPSILON = 1e-06


def one_axis_at_a_time(x, axes):
    for axis in axes:
        x = lax.psum(x, axis)
    return x


def per_device(grad_pooled, bag_len, lookup_slot, slot_row, weights, accum):
    lane_count = lax.axis_size(LANE)
    group_count = lax.axis_size(GRP)
    number_slots = group_count * SLOTS_PEER
    batch_rows, table_count, embed_width = grad_pooled.shape
    tables_here = table_count // lane_count
    bag_depth = lookup_slot.shape[2]
    scaled = (grad_pooled.astype(jnp.float32) / bag_len.astype(jnp.float32)[:, :, None]).astype(
        jnp.bfloat16
    )
    arrived = lax.all_to_all(scaled, LANE, split_axis=1, concat_axis=0, tiled=True)
    values = arrived.reshape(lane_count, batch_rows * tables_here, embed_width)
    slot_marks = lookup_slot.reshape(lane_count, batch_rows * tables_here, bag_depth)
    numbers = lax.broadcasted_iota(jnp.int32, (1, number_slots, 1, 1), 1)
    counts = jnp.sum(slot_marks[:, None, :, :] == numbers, axis=-1, dtype=jnp.int32).astype(
        jnp.bfloat16
    )
    partial_value = jnp.einsum(
        "lsk,lke->lse", counts, values, preferred_element_type=jnp.float32
    ).astype(jnp.bfloat16)
    slot_sum = jnp.sum(partial_value.astype(jnp.float32), axis=0).astype(jnp.bfloat16)
    outgoing = slot_sum.reshape(group_count, SLOTS_PEER, embed_width)
    incoming = lax.all_to_all(outgoing, GRP, split_axis=0, concat_axis=0, tiled=True).reshape(
        number_slots, embed_width
    )
    targets = slot_row.reshape(1, number_slots)
    local_rows = accum.shape[0] * accum.shape[1]
    row_ids = lax.broadcasted_iota(jnp.int32, (local_rows, 1), 0)
    placing = (row_ids == targets).astype(jnp.bfloat16)
    row_grad = jnp.dot(placing, incoming, preferred_element_type=jnp.float32)
    square_mean = jnp.mean(row_grad * row_grad, axis=1)
    norm_total = one_axis_at_a_time(embed_width * jnp.sum(square_mean), GRP_LANE)
    clip_limit = 0.5 * math.sqrt(group_count * lane_count * number_slots * embed_width)
    clip_factor = clip_limit / jnp.maximum(jnp.sqrt(norm_total), clip_limit)
    new_accum = accum + clip_factor * clip_factor * square_mean.reshape(accum.shape)
    step_rows = LEARN_RATE * clip_factor * row_grad.reshape(weights.shape)
    new_weights = weights - step_rows / (jnp.sqrt(new_accum)[:, :, None] + EPSILON)
    return (new_weights, new_accum)


def solution(mesh):
    torus = Mesh(mesh.devices.reshape(12, 8, 4, 2), ("grp_0", "grp_1", "lane_0", "lane_1"))
    in_specs = (
        P(GRP_LANE, None, None),
        P(GRP_LANE, None),
        P(GRP, LANE, None),
        P(GRP, LANE, None, None),
        P(LANE, GRP, None),
        P(LANE, GRP),
    )
    out_specs = (P(LANE, GRP, None), P(LANE, GRP))
    return jax.shard_map(
        per_device, mesh=torus, in_specs=in_specs, out_specs=out_specs, check_vma=False
    )
```

profile of v0, /device:TPU:1, one launch (start us, length us, event | category | flops | bytes accessed | tf_op | source)
XLA Modules:
  0.0 140.2 jit_solution(11512259977400811803)
XLA Ops:
  0.6 0.7 convert_element_type.24
  1.4 3.4 %divide_convert_fusion = bf16[128,32,256]{2,0,1:T(8,128)(2,1)} fusion(bf16[128,32,256]{2,1,0:T(8,128)(2,1)} %param.6, f32[128,32]{0,1:T(8,128)S(1)} %convert_element_type.24), kind=kLoop, calls=%fused_computation.2 | loop fusion | flops 3145728 | bytes 4210688 | tf_op jit(solution)/shard_map/convert_element_type | solution.py:32
  4.7 0.0 copy-start.1
  4.7 14.8 %all-to-all-start = ((bf16[128,32,256]{2,0,1:T(8,128)(2,1)}), bf16[128,32,256]{2,0,1:T(8,128)(2,1)}, u32[]{:S(2)}, u32[]{:S(2)}) async-start(bf16[128,32,256]{2,0,1:T(8,128)(2,1)} %divide_convert_fusion), calls=%async_computation | async-start | bytes 4194304 | tf_op jit(solution)/shard_map/all_to_all | solution.py:35
  19.6 0.0 copy-done.1
  19.6 0.8 copy.19
  20.4 0.6 copy.20
  21.0 8.8 %convert_reduce_fusion = s32[8,192,512]{2,1,0:T(8,128)S(1)} fusion(s32[8,512,8]{1,2,0:T(8,128)S(1)} %copy.20), kind=kLoop, calls=%fused_computation | loop fusion | flops 18087936 | bytes 3276800 | tf_op jit(solution)/shard_map/reduce_sum | solution.py:39
  29.8 16.1 %all-to-all-done = bf16[128,32,256]{2,0,1:T(8,128)(2,1)} async-done(((bf16[128,32,256]{2,0,1:T(8,128)(2,1)}), bf16[128,32,256]{2,0,1:T(8,128)(2,1)}, u32[]{:S(2)}, u32[]{:S(2)}) %all-to-all-start) | async-done | bytes 2097184 | tf_op jit(solution)/shard_map/all_to_all | solution.py:35
  45.9 4.5 %copy.25 = bf16[128,8,4,256]{3,2,0,1:T(4,128)(2,1)} copy(bf16[128,8,4,256]{3,0,2,1:T(8,128)(2,1)} %bitcast.1) | data formatting | bytes 4194304 | tf_op jit(solution)/shard_map/all_to_all | solution.py:35
  50.4 4.0 %reshape.27 = bf16[8,512,256]{2,1,0:T(8,128)(2,1)} reshape(bf16[8,128,4,256]{3,2,1,0:T(4,128)(2,1)} %bitcast.10) | data formatting | bytes 4194304 | tf_op jit(solution)/shard_map/reshape | solution.py:36
  54.4 0.0 copy-start.3
  54.4 0.0 copy-start.2
  54.4 2.2 %fusion.5 = bf16[192,256]{1,0:T(8,128)(2,1)S(1)} fusion(bf16[8,512,256]{2,1,0:T(8,128)(2,1)} %reshape.27, s32[8,192,512]{2,1,0:T(8,128)S(1)} %convert_reduce_fusion), kind=kOutput, calls=%fused_computation.7 | convolution fusion | flops 404176896 | bytes 5341184 | tf_op jit(solution)/shard_map/lsk,lke->lse/dot_general | solution.py:42
  56.6 0.0 copy-start
  56.6 0.7 reshape.28
  57.3 12.8 %all-to-all-start.1 = ((bf16[96,2,256]{2,1,0:T(2,128)(2,1)}), bf16[96,2,256]{2,1,0:T(2,128)(2,1)S(1)}, u32[]{:S(2)}, u32[]{:S(2)}) async-start(bf16[96,2,256]{2,1,0:T(2,128)(2,1)} %reshape.28), calls=%async_computation.1 | async-start | bytes 196608 | tf_op jit(solution)/shard_map/all_to_all | solution.py:47
  70.1 0.0 copy-done.3
  70.1 0.1 copy.18
  70.2 0.1 eq.31
  70.3 13.2 %all-to-all-done.1 = bf16[96,2,256]{2,1,0:T(2,128)(2,1)S(1)} async-done(((bf16[96,2,256]{2,1,0:T(2,128)(2,1)}), bf16[96,2,256]{2,1,0:T(2,128)(2,1)S(1)}, u32[]{:S(2)}, u32[]{:S(2)}) %all-to-all-start.1) | async-done | bytes 98336 | tf_op jit(solution)/shard_map/all_to_all | solution.py:47
  83.6 0.4 multiply_reduce_fusion
  84.0 0.6 multiply_reduce_fusion.1
  85.3 17.1 %psum.28 = f32[]{:T(128)} all-reduce(f32[]{:T(128)S(6)} %mul.30), channel_id=1, replica_groups=mesh['grp_0'=12,'grp_1'=8,'lane_0'=4,'lane_1'=2] {'grp_0'}, use_global_device_ids=true, to_apply=%region_4.0 | all-reduce | flops 1 | bytes 8 | tf_op jit(solution)/shard_map/psum | solution.py:21
  102.4 11.9 %psum.29 = f32[]{:T(128)} all-reduce(f32[]{:T(128)} %psum.28), channel_id=1, replica_groups=mesh['grp_0'=12,'grp_1'=8,'lane_0'=4,'lane_1'=2] {'grp_1'}, use_global_device_ids=true, to_apply=%region_5.0 | all-reduce | flops 1 | bytes 8 | tf_op jit(solution)/shard_map/psum | solution.py:21
  114.2 7.5 %psum.30 = f32[]{:T(128)} all-reduce(f32[]{:T(128)} %psum.29), channel_id=1, replica_groups=mesh['grp_0'=12,'grp_1'=8,'lane_0'=4,'lane_1'=2] {'lane_0'}, use_global_device_ids=true, to_apply=%region_6.0 | all-reduce | flops 1 | bytes 8 | tf_op jit(solution)/shard_map/psum | solution.py:21
  121.7 15.8 %psum.31 = f32[]{:T(128)} all-reduce(f32[]{:T(128)} %psum.30), channel_id=1, replica_groups=mesh['grp_0'=12,'grp_1'=8,'lane_0'=4,'lane_1'=2] {'lane_1'}, use_global_device_ids=true, to_apply=%region_7.0 | all-reduce | flops 1 | bytes 8 | tf_op jit(solution)/shard_map/psum | solution.py:21
  138.3 0.0 copy-done.2
  138.3 0.6 sqrt_add_fusion
  138.9 0.1 broadcast_multiply_fusion
  139.0 0.0 copy-done
  139.0 1.2 divide_subtract_fusion
  (3 shorter events, 0.1 us)
Async XLA Ops:
  4.7 14.8 %copy-start.1 = (s32[1024,4,8]{0,2,1:T(8,128)S(1)}, s32[1024,4,8]{0,2,1:T(8,128)}, u32[]{:S(2)}) copy-start(s32[1024,4,8]{0,2,1:T(8,128)} %param.8) | copy-start | bytes 393220
  4.7 41.2 %all-to-all-start = ((bf16[128,32,256]{2,0,1:T(8,128)(2,1)}), bf16[128,32,256]{2,0,1:T(8,128)(2,1)}, u32[]{:S(2)}, u32[]{:S(2)}) async-start(bf16[128,32,256]{2,0,1:T(8,128)(2,1)} %divide_convert_fusion), calls=%async_computation | async-start | bytes 4194304 | tf_op jit(solution)/shard_map/all_to_all | solution.py:35
  54.4 15.7 %copy-start.3 = (s32[1,1,96,2]{2,3,1,0:T(2,128)S(1)}, s32[1,1,96,2]{2,3,1,0:T(2,128)}, u32[]{:S(2)}) copy-start(s32[1,1,96,2]{2,3,1,0:T(2,128)} %param.9) | copy-start | bytes 2308
  54.4 84.0 %copy-start.2 = (f32[4,256]{1,0:T(4,128)S(1)}, f32[4,256]{1,0:T(4,128)}, u32[]{:S(2)}) copy-start(f32[4,256]{1,0:T(4,128)} %param.11) | copy-start | bytes 12292
  56.6 82.4 %copy-start = (f32[4,256,256]{2,1,0:T(8,128)S(1)}, f32[4,256,256]{2,1,0:T(8,128)}, u32[]{:S(2)}) copy-start(f32[4,256,256]{2,1,0:T(8,128)} %param.10) | copy-start | bytes 3145732
  57.3 26.3 %all-to-all-start.1 = ((bf16[96,2,256]{2,1,0:T(2,128)(2,1)}), bf16[96,2,256]{2,1,0:T(2,128)(2,1)S(1)}, u32[]{:S(2)}, u32[]{:S(2)}) async-start(bf16[96,2,256]{2,1,0:T(2,128)(2,1)} %reshape.28), calls=%async_computation.1 | async-start | bytes 196608 | tf_op jit(solution)/shard_map/all_to_all | solution.py:47
where the time goes:
time: 141 us; the launch traced here: 140 us
  blocking collectives  52.3 us (37%)
  waiting for transfers between devices  29.4 us (21%)
  starting transfers between devices  27.6 us (20%)
  other arithmetic  15.4 us (11%)
  local copies, waits for them, and re-layouts  10.9 us (8%)
  matrix products  2.59 us (2%)
  between operations  2.11 us (1%)
    psum x4, blocking collectives, one_axis_at_a_time(): x = lax.psum(x, axis)  52.3 us
    all_to_all x1, waiting for transfers between devices, per_device(): lax.all_to_all(scaled, LANE, split_axis=1, concat_axis=0, tiled=True)  16.1 us
    all_to_all x1, starting transfers between devices, per_device(): lax.all_to_all(scaled, LANE, split_axis=1, concat_axis=0, tiled=True)  14.8 us
    all_to_all x1, waiting for transfers between devices, per_device(): lax.all_to_all(outgoing, GRP, split_axis=0, concat_axis=0, tiled=True)  13.2 us
    all_to_all x1, starting transfers between devices, per_device(): lax.all_to_all(outgoing, GRP, split_axis=0, concat_axis=0, tiled=True)  12.8 us
    reduce_sum x1, other arithmetic, per_device(): jnp.sum(slot_marks[:, None, :, :] == numbers, axis=-1, dtype=jnp.int32)  8.81 us
    all_to_all x1, local copies, waits for them, and re-layouts, per_device(): lax.all_to_all(scaled, LANE, split_axis=1, concat_axis=0, tiled=True)  4.51 us
    reshape x1, local copies, waits for them, and re-layouts, per_device(): values = arrived.reshape(lane_count, batch_rows * tables_here, embed_width)  3.97 us
  transfers between devices with their start and end apart: 2, of which 2 were waited for; matrix products, arithmetic and copies ran while one was open for 7% of the time, Pallas kernels for 0%

commit v1 on v0

--- a/solution.py
+++ b/solution.py
@@ -16,10 +16,15 @@
 EPSILON = 1e-06
 
 
-def one_axis_at_a_time(x, axes):
-    for axis in axes:
-        x = lax.psum(x, axis)
-    return x
+def gathered(x, axes):
+    count = lax.axis_size(axes)
+    copies = jnp.broadcast_to(x.reshape(1, 1, 128), (count, 1, 128))
+    return lax.all_to_all(copies, axes, split_axis=0, concat_axis=0, tiled=True)
+
+
+def sum_over_all(row):
+    row = jnp.sum(gathered(row, ("grp_0", "lane_1")), axis=0)
+    return jnp.sum(gathered(row, ("grp_1", "lane_0")))
 
 
 def per_device(grad_pooled, bag_len, lookup_slot, slot_row, weights, accum):
@@ -53,7 +58,8 @@
     placing = (row_ids == targets).astype(jnp.bfloat16)
     row_grad = jnp.dot(placing, incoming, preferred_element_type=jnp.float32)
     square_mean = jnp.mean(row_grad * row_grad, axis=1)
-    norm_total = one_axis_at_a_time(embed_width * jnp.sum(square_mean), GRP_LANE)
+    norm_row = jnp.sum(square_mean.reshape(-1, 128), axis=0)
+    norm_total = embed_width * sum_over_all(norm_row)
     clip_limit = 0.5 * math.sqrt(group_count * lane_count * number_slots * embed_width)
     clip_factor = clip_limit / jnp.maximum(jnp.sqrt(norm_total), clip_limit)
     new_accum = accum + clip_factor * clip_factor * square_mean.reshape(accum.shape)

time: 141 us -> 114 us (0.81)
  blocking collectives: 52.3 us -> 26.3 us
    psum x4 -> x0, blocking collectives: 52.3 us -> none  [one_axis_at_a_time(): x = lax.psum(x, axis)]
    all_to_all x0 -> x2, blocking collectives: none -> 26.3 us  [gathered(): return lax.all_to_all(copies, axes, split_axis=0, concat_axis=0, tiled=True)]
  transfers between devices with their start and end apart: 2 -> 2, of which waited for: 2 -> 2; matrix products, arithmetic and copies ran while one was open for 7% -> 9% of each run, Pallas kernels for 0% -> 0%
where the time goes in v1:
time: 114 us
  waiting for transfers between devices  29.4 us (26%)
  starting transfers between devices  27.6 us (24%)
  blocking collectives  26.3 us (23%)
  other arithmetic  15.4 us (14%)
  local copies, waits for them, and re-layouts  10.9 us (10%)
  matrix products  2.59 us (2%)
  between operations  1.46 us (1%)
    all_to_all x2, blocking collectives, gathered(): return lax.all_to_all(copies, axes, split_axis=0, concat_axis=0, tiled=True)  26.3 us
    all_to_all x1, waiting for transfers between devices, per_device(): lax.all_to_all(scaled, LANE, split_axis=1, concat_axis=0, tiled=True)  16.1 us
    all_to_all x1, starting transfers between devices, per_device(): lax.all_to_all(scaled, LANE, split_axis=1, concat_axis=0, tiled=True)  14.8 us
    all_to_all x1, waiting for transfers between devices, per_device(): lax.all_to_all(outgoing, GRP, split_axis=0, concat_axis=0, tiled=True)  13.2 us
    all_to_all x1, starting transfers between devices, per_device(): lax.all_to_all(outgoing, GRP, split_axis=0, concat_axis=0, tiled=True)  12.8 us
    reduce_sum x1, other arithmetic, per_device(): jnp.sum(slot_marks[:, None, :, :] == numbers, axis=-1, dtype=jnp.int32)  8.81 us
    all_to_all x1, local copies, waits for them, and re-layouts, per_device(): lax.all_to_all(scaled, LANE, split_axis=1, concat_axis=0, tiled=True)  4.51 us
    reshape x1, local copies, waits for them, and re-layouts, per_device(): values = arrived.reshape(lane_count, batch_rows * tables_here, embed_width)  3.97 us
  transfers between devices with their start and end apart: 2, of which 2 were waited for; matrix products, arithmetic and copies ran while one was open for 9% of the time, Pallas kernels for 0%

profile of v1, /device:TPU:1, one launch (start us, length us, event | category | flops | bytes accessed | tf_op | source)
XLA Modules:
  0.0 113.6 jit_solution(9887667445995186298)
XLA Ops:
  0.6 0.7 convert_element_type.24
  1.4 3.4 %divide_convert_fusion = bf16[128,32,256]{2,0,1:T(8,128)(2,1)} fusion(bf16[128,32,256]{2,1,0:T(8,128)(2,1)} %param.6, f32[128,32]{0,1:T(8,128)S(1)} %convert_element_type.24), kind=kLoop, calls=%fused_computation.2 | loop fusion | flops 3145728 | bytes 4210688 | tf_op jit(solution)/shard_map/convert_element_type | solution.py:37
  4.7 0.0 copy-start.1
  4.7 14.8 %all-to-all-start = ((bf16[128,32,256]{2,0,1:T(8,128)(2,1)}), bf16[128,32,256]{2,0,1:T(8,128)(2,1)}, u32[]{:S(2)}, u32[]{:S(2)}) async-start(bf16[128,32,256]{2,0,1:T(8,128)(2,1)} %divide_convert_fusion), calls=%async_computation | async-start | bytes 4194304 | tf_op jit(solution)/shard_map/all_to_all | solution.py:40
  19.6 0.0 copy-done.1
  19.6 0.8 copy.24
  20.4 0.6 copy.25
  21.0 8.8 %convert_reduce_fusion = s32[8,192,512]{2,1,0:T(8,128)S(1)} fusion(s32[8,512,8]{1,2,0:T(8,128)S(1)} %copy.25), kind=kLoop, calls=%fused_computation | loop fusion | flops 18087936 | bytes 3276800 | tf_op jit(solution)/shard_map/reduce_sum | solution.py:44
  29.8 16.1 %all-to-all-done = bf16[128,32,256]{2,0,1:T(8,128)(2,1)} async-done(((bf16[128,32,256]{2,0,1:T(8,128)(2,1)}), bf16[128,32,256]{2,0,1:T(8,128)(2,1)}, u32[]{:S(2)}, u32[]{:S(2)}) %all-to-all-start) | async-done | bytes 2097184 | tf_op jit(solution)/shard_map/all_to_all | solution.py:40
  45.9 4.5 %copy.32 = bf16[128,8,4,256]{3,2,0,1:T(4,128)(2,1)} copy(bf16[128,8,4,256]{3,0,2,1:T(8,128)(2,1)} %bitcast.1) | data formatting | bytes 4194304 | tf_op jit(solution)/shard_map/all_to_all | solution.py:40
  50.4 4.0 %reshape.41 = bf16[8,512,256]{2,1,0:T(8,128)(2,1)} reshape(bf16[8,128,4,256]{3,2,1,0:T(4,128)(2,1)} %bitcast.14) | data formatting | bytes 4194304 | tf_op jit(solution)/shard_map/reshape | solution.py:41
  54.4 0.0 copy-start.3
  54.4 0.0 copy-start.2
  54.4 2.2 %fusion.5 = bf16[192,256]{1,0:T(8,128)(2,1)S(1)} fusion(bf16[8,512,256]{2,1,0:T(8,128)(2,1)} %reshape.41, s32[8,192,512]{2,1,0:T(8,128)S(1)} %convert_reduce_fusion), kind=kOutput, calls=%fused_computation.7 | convolution fusion | flops 404176896 | bytes 5341184 | tf_op jit(solution)/shard_map/lsk,lke->lse/dot_general | solution.py:47
  56.6 0.0 copy-start
  56.6 0.7 reshape.42
  57.3 12.8 %all-to-all-start.1 = ((bf16[96,2,256]{2,1,0:T(2,128)(2,1)}), bf16[96,2,256]{2,1,0:T(2,128)(2,1)S(1)}, u32[]{:S(2)}, u32[]{:S(2)}) async-start(bf16[96,2,256]{2,1,0:T(2,128)(2,1)} %reshape.42), calls=%async_computation.1 | async-start | bytes 196608 | tf_op jit(solution)/shard_map/all_to_all | solution.py:52
  70.1 0.0 copy-done.3
  70.1 0.1 copy.23
  70.2 0.1 eq.31
  70.3 13.2 %all-to-all-done.1 = bf16[96,2,256]{2,1,0:T(2,128)(2,1)S(1)} async-done(((bf16[96,2,256]{2,1,0:T(2,128)(2,1)}), bf16[96,2,256]{2,1,0:T(2,128)(2,1)S(1)}, u32[]{:S(2)}, u32[]{:S(2)}) %all-to-all-start.1) | async-done | bytes 98336 | tf_op jit(solution)/shard_map/all_to_all | solution.py:52
  83.6 0.4 multiply_reduce_fusion
  84.0 14.6 %all_to_all.30 = f32[24,1,128]{2,1,0:T(1,128)S(1)} all-to-all(f32[24,1,128]{2,1,0:T(1,128)S(1)} %broadcast_in_dim.4), channel_id=1, replica_groups=mesh['grp_0'=12,'grp_1'=8,'lane_0'=4,'lane_1'=2] {'grp_0','lane_1'}, dimensions={0} | all-to-all | bytes 24576 | tf_op jit(solution)/shard_map/all_to_all | solution.py:22
  98.6 11.7 %all_to_all.31 = f32[32,1,128]{2,1,0:T(1,128)S(1)} all-to-all(f32[32,1,128]{2,1,0:T(1,128)S(1)} %broadcast_in_dim.5), channel_id=1, replica_groups=mesh['grp_0'=12,'grp_1'=8,'lane_0'=4,'lane_1'=2] {'grp_1','lane_0'}, dimensions={0} | all-to-all | bytes 32768 | tf_op jit(solution)/shard_map/all_to_all | solution.py:22
  110.3 0.6 reduce_sum.62
  111.7 0.0 copy-done.2
  111.7 0.6 sqrt_add_fusion
  112.3 0.1 broadcast_multiply_fusion
  112.4 0.0 copy-done
  112.4 1.2 %divide_subtract_fusion = f32[4,256,256]{2,1,0:T(8,128)} fusion(f32[4,256,256]{2,1,0:T(8,128)S(1)} %copy-done, f32[4,256,256]{2,1,0:T(8,128)S(1)} %bitcast.16, f32[4,256]{1,0:T(4,128)S(1)} %get-tuple-element.2), kind=kLoop, calls=%fused_computation.8 | loop fusion | flops 524288 | bytes 3149824 | tf_op jit(solution)/shard_map/sub | solution.py:67
  (7 shorter events, 0.1 us)
Async XLA Ops:
  4.7 14.8 %copy-start.1 = (s32[1024,4,8]{0,2,1:T(8,128)S(1)}, s32[1024,4,8]{0,2,1:T(8,128)}, u32[]{:S(2)}) copy-start(s32[1024,4,8]{0,2,1:T(8,128)} %param.8) | copy-start | bytes 393220
  4.7 41.2 %all-to-all-start = ((bf16[128,32,256]{2,0,1:T(8,128)(2,1)}), bf16[128,32,256]{2,0,1:T(8,128)(2,1)}, u32[]{:S(2)}, u32[]{:S(2)}) async-start(bf16[128,32,256]{2,0,1:T(8,128)(2,1)} %divide_convert_fusion), calls=%async_computation | async-start | bytes 4194304 | tf_op jit(solution)/shard_map/all_to_all | solution.py:40
  54.4 15.7 %copy-start.3 = (s32[1,1,96,2]{2,3,1,0:T(2,128)S(1)}, s32[1,1,96,2]{2,3,1,0:T(2,128)}, u32[]{:S(2)}) copy-start(s32[1,1,96,2]{2,3,1,0:T(2,128)} %param.9) | copy-start | bytes 2308
  54.4 57.3 %copy-start.2 = (f32[4,256]{1,0:T(4,128)S(1)}, f32[4,256]{1,0:T(4,128)}, u32[]{:S(2)}) copy-start(f32[4,256]{1,0:T(4,128)} %param.11) | copy-start | bytes 12292
  56.6 55.8 %copy-start = (f32[4,256,256]{2,1,0:T(8,128)S(1)}, f32[4,256,256]{2,1,0:T(8,128)}, u32[]{:S(2)}) copy-start(f32[4,256,256]{2,1,0:T(8,128)} %param.10) | copy-start | bytes 3145732
  57.3 26.3 %all-to-all-start.1 = ((bf16[96,2,256]{2,1,0:T(2,128)(2,1)}), bf16[96,2,256]{2,1,0:T(2,128)(2,1)S(1)}, u32[]{:S(2)}, u32[]{:S(2)}) async-start(bf16[96,2,256]{2,1,0:T(2,128)(2,1)} %reshape.42), calls=%async_computation.1 | async-start | bytes 196608 | tf_op jit(solution)/shard_map/all_to_all | solution.py:52

commit v2 on v1

--- a/solution.py
+++ b/solution.py
@@ -3,8 +3,11 @@
 import jax
 import jax.numpy as jnp
 from jax import lax
+from jax.experimental import pallas as pl
+from jax.experimental.pallas import tpu as pltpu
 from jax.sharding import Mesh
 from jax.sharding import PartitionSpec as P
+
 
 SLOTS_PEER = 2
 LANE = ("lane_0", "lane_1")
@@ -16,10 +19,13 @@
 EPSILON = 1e-06
 
 
+def exchange(x, axes):
+    return lax.all_to_all(x, axes, split_axis=0, concat_axis=0, tiled=True)
+
+
 def gathered(x, axes):
     count = lax.axis_size(axes)
-    copies = jnp.broadcast_to(x.reshape(1, 1, 128), (count, 1, 128))
-    return lax.all_to_all(copies, axes, split_axis=0, concat_axis=0, tiled=True)
+    return exchange(jnp.broadcast_to(x.reshape(1, 1, 128), (count, 1, 128)), axes)
 
 
 def sum_over_all(row):
@@ -27,31 +33,113 @@
     return jnp.sum(gathered(row, ("grp_1", "lane_0")))
 
 
+VMEM = pl.BlockSpec(memory_space=pltpu.VMEM)
+
+
+def kernel_call(kernel, out_shape, flops, *args):
+    moved = sum(x.size * x.dtype.itemsize for x in (*args, out_shape))
+    return pl.pallas_call(
+        kernel,
+        out_shape=out_shape,
+        in_specs=[VMEM] * len(args),
+        out_specs=VMEM,
+        compiler_params=pltpu.CompilerParams(vmem_limit_bytes=16 * 1024 * 1024),
+        cost_estimate=pl.CostEstimate(flops=flops, bytes_accessed=moved, transcendentals=0),
+    )(*args)
+
+
+def marks_kernel(slot_ref, out_ref):
+    chips, cores, tables, _, samples = out_ref.shape
+    for chip in range(chips):
+        for core in range(cores):
+            start = (chip * cores + core) * samples
+            for table in range(tables):
+                out_ref[chip, core, table] = slot_ref[table, :, start : start + samples].astype(
+                    out_ref.dtype
+                )
+
+
+def counts_kernel(marks_ref, out_ref):
+    chips, cores, tables, depth, samples = marks_ref.shape
+    slots = out_ref.shape[1]
+    numbers = lax.broadcasted_iota(jnp.int32, (slots, samples), 0).astype(jnp.bfloat16)
+    one, zero = jnp.bfloat16(1), jnp.bfloat16(0)
+    for chip in range(chips):
+        for core in range(cores):
+            for table in range(tables):
+                total = None
+                for position in range(depth):
+                    mark = marks_ref[chip, core, table, position : position + 1, :]
+                    hit = jnp.where(numbers == mark, one, zero)
+                    total = hit if total is None else total + hit
+                start = (core * tables + table) * samples
+                out_ref[chip, :, start : start + samples] = total
+
+
+def sums_kernel(counts_ref, own_ref, pair_ref, out_ref):
+    chips, _, terms = counts_ref.shape
+    cores = lax.axis_size("lane_1")
+    tables = own_ref.shape[0] // (chips * cores)
+    width = own_ref.shape[2]
+    core = lax.axis_index("lane_1")
+    half = terms // cores
+    for chip in range(chips):
+        start = (chip * cores + core) * tables
+        mine = pl.multiple_of(core * half, half)
+        other = pl.multiple_of((1 - core) * half, half)
+        out_ref[chip] = (
+            jnp.dot(
+                counts_ref[chip, :, pl.ds(mine, half)],
+                own_ref[pl.ds(start, tables)].reshape(half, width),
+                preferred_element_type=jnp.float32,
+            )
+            + jnp.dot(
+                counts_ref[chip, :, pl.ds(other, half)],
+                pair_ref[pl.ds(start, tables)].reshape(half, width),
+                preferred_element_type=jnp.float32,
+            )
+        ).astype(out_ref.dtype)
+
+
 def per_device(grad_pooled, bag_len, lookup_slot, slot_row, weights, accum):
     lane_count = lax.axis_size(LANE)
+    chips, cores = lax.axis_size("lane_0"), lax.axis_size("lane_1")
     group_count = lax.axis_size(GRP)
     number_slots = group_count * SLOTS_PEER
     batch_rows, table_count, embed_width = grad_pooled.shape
     tables_here = table_count // lane_count
     bag_depth = lookup_slot.shape[2]
-    scaled = (grad_pooled.astype(jnp.float32) / bag_len.astype(jnp.float32)[:, :, None]).astype(
-        jnp.bfloat16
+    marks = kernel_call(
+        marks_kernel,
+        jax.ShapeDtypeStruct((chips, cores, tables_here, bag_depth, batch_rows), jnp.bfloat16),
+        lookup_slot.size,
+        lookup_slot.transpose(1, 2, 0),
     )
-    arrived = lax.all_to_all(scaled, LANE, split_axis=1, concat_axis=0, tiled=True)
-    values = arrived.reshape(lane_count, batch_rows * tables_here, embed_width)
-    slot_marks = lookup_slot.reshape(lane_count, batch_rows * tables_here, bag_depth)
-    numbers = lax.broadcasted_iota(jnp.int32, (1, number_slots, 1, 1), 1)
-    counts = jnp.sum(slot_marks[:, None, :, :] == numbers, axis=-1, dtype=jnp.int32).astype(
-        jnp.bfloat16
+    marks = exchange(marks, "lane_0")
+    scaled = (
+        grad_pooled.astype(jnp.float32) * (1.0 / bag_len.astype(jnp.float32))[:, :, None]
+    ).astype(jnp.bfloat16)
+    scaled = scaled.transpose(1, 0, 2)
+    pair = lax.ppermute(scaled, "lane_1", [(0, 1), (1, 0)])
+    terms = cores * tables_here * batch_rows
+    counts = kernel_call(
+        counts_kernel,
+        jax.ShapeDtypeStruct((chips, number_slots, terms), jnp.bfloat16),
+        chips * number_slots * terms * bag_depth,
+        marks,
     )
-    partial_value = jnp.einsum(
-        "lsk,lke->lse", counts, values, preferred_element_type=jnp.float32
-    ).astype(jnp.bfloat16)
+    partial_value = kernel_call(
+        sums_kernel,
+        jax.ShapeDtypeStruct((chips, number_slots, embed_width), jnp.bfloat16),
+        2 * chips * number_slots * terms * embed_width,
+        counts,
+        scaled,
+        pair,
+    )
+    partial_value = exchange(partial_value, "lane_0")
     slot_sum = jnp.sum(partial_value.astype(jnp.float32), axis=0).astype(jnp.bfloat16)
     outgoing = slot_sum.reshape(group_count, SLOTS_PEER, embed_width)
-    incoming = lax.all_to_all(outgoing, GRP, split_axis=0, concat_axis=0, tiled=True).reshape(
-        number_slots, embed_width
-    )
+    incoming = exchange(outgoing, GRP).reshape(number_slots, embed_width)
     targets = slot_row.reshape(1, number_slots)
     local_rows = accum.shape[0] * accum.shape[1]
     row_ids = lax.broadcasted_iota(jnp.int32, (local_rows, 1), 0)

time: 114 us -> 94.5 us (0.83)
  blocking collectives: 26.3 us -> 44.1 us
  waiting for transfers between devices: 29.4 us -> 13.3 us
  local copies, waits for them, and re-layouts: 10.9 us -> 1.02 us
  other arithmetic: 15.4 us -> 5.77 us
  matrix products: 2.59 us -> 0.4 us
  Pallas kernels: 0 us -> 1.99 us
  starting transfers between devices: 27.6 us -> 26 us
    all_to_all x2 -> x4, blocking collectives: 26.3 us -> 44.1 us  [exchange(): return lax.all_to_all(x, axes, split_axis=0, concat_axis=0, tiled=True)]
    all_to_all x2 -> x1, waiting for transfers between devices: 29.4 us -> 13.3 us  [exchange(): return lax.all_to_all(x, axes, split_axis=0, concat_axis=0, tiled=True)]
    all_to_all x2 -> x1, starting transfers between devices: 27.6 us -> 13.6 us  [exchange(): return lax.all_to_all(x, axes, split_axis=0, concat_axis=0, tiled=True)]
    ppermute x0 -> x1, starting transfers between devices: none -> 12.4 us  [per_device(): pair = lax.ppermute(scaled, 'lane_1', [(0, 1), (1, 0)])]
    reduce_sum x1, other arithmetic: 8.81 us -> 0.06 us  [per_device(): jnp.sum(partial_value.astype(jnp.float32), axis=0).astype(jnp.bfloat16)]
    all_to_all x1 -> x0, local copies, waits for them, and re-layouts: 4.51 us -> none  [per_device(): lax.all_to_all(scaled, LANE, split_axis=1, concat_axis=0, tiled=True)]
    convert_element_type x2 -> x0, other arithmetic: 4.1 us -> none  [the longest x1 3.38 us: per_device(): (grad_pooled.astype(jnp.float32) / bag_len.astype(jnp.float32)[:, :, None...]
    reshape x2 -> x1, local copies, waits for them, and re-layouts: 4.01 us -> 0.04 us  [per_device(): incoming = exchange(outgoing, GRP).reshape(number_slots, embed_width)]
  transfers between devices with their start and end apart: 2 -> 2, of which waited for: 2 -> 1; matrix products, arithmetic and copies ran while one was open for 9% -> 0% of each run, Pallas kernels for 0% -> 1%
where the time goes in v2:
time: 94.5 us; the launch traced here: 94 us
  blocking collectives  44.1 us (47%)
  starting transfers between devices  26 us (28%)
  waiting for transfers between devices  13.3 us (14%)
  other arithmetic  5.77 us (6%)
  Pallas kernels  1.99 us (2%)
  between operations  1.5 us (2%)
  local copies, waits for them, and re-layouts  1.02 us (1%)
    all_to_all x4, blocking collectives, exchange(): return lax.all_to_all(x, axes, split_axis=0, concat_axis=0, tiled=True)  44.1 us
    all_to_all x1, starting transfers between devices, exchange(): return lax.all_to_all(x, axes, split_axis=0, concat_axis=0, tiled=True)  13.6 us
    all_to_all x1, waiting for transfers between devices, exchange(): return lax.all_to_all(x, axes, split_axis=0, concat_axis=0, tiled=True)  13.3 us
    ppermute x1, starting transfers between devices, per_device(): pair = lax.ppermute(scaled, 'lane_1', [(0, 1), (1, 0)])  12.4 us
    transpose x1, other arithmetic, per_device(): scaled = scaled.transpose(1, 0, 2)  2.48 us
    pallas_call x3, Pallas kernels, kernel_call(): pl.pallas_call(kernel, out_shape=out_shape, in_specs=[VMEM] * len(args),...  1.99 us
  transfers between devices with their start and end apart: 2, of which 1 were waited for; matrix products, arithmetic and copies ran while one was open for 0% of the time, Pallas kernels for 1%

profile of v2, /device:TPU:1, one launch (start us, length us, event | category | flops | bytes accessed | tf_op | source)
XLA Modules:
  0.0 94.0 jit_solution(15789114664954615171)
XLA Ops:
  0.6 0.7 convert_divide_fusion
  1.4 0.0 copy-start
  1.4 2.5 %fusion.own_ref = bf16[32,128,256]{2,1,0:T(8,128)(2,1)S(1)} fusion(bf16[128,32,256]{2,1,0:T(8,128)(2,1)} %param.6, f32[128,32]{0,1:T(8,128)S(1)} %convert_divide_fusion), kind=kLoop, calls=%fused_computation.1 | loop fusion | flops 3145728 | bytes 4210688 | tf_op jit(solution)/shard_map/transpose | solution.py:122
  3.8 12.4 %collective-permute-start = (bf16[32,128,256]{2,1,0:T(8,128)(2,1)S(1)}, bf16[32,128,256]{2,1,0:T(8,128)(2,1)S(1)}, u32[]{:S(2)}, u32[]{:S(2)}) collective-permute-start(bf16[32,128,256]{2,1,0:T(8,128)(2,1)S(1)} %fusion.own_ref), channel_id=1, source_target_pairs={{0,1},{1,0},{2,3},{3,2},{4,5},{5,4},{6,7},{7,6},{8,9},{9,8},{10,11... | collective-permute-start | bytes 6291464 | tf_op jit(solution)/shard_map/ppermute | solution.py:123
  16.2 0.0 copy-done
  16.3 6.9 %all_to_all.25.marks_ref = bf16[4,2,4,8,128]{4,3,2,1,0:T(8,128)(2,1)S(1)} all-to-all(bf16[4,2,4,8,128]{4,3,2,1,0:T(8,128)(2,1)S(1)} %shard_map.77), channel_id=1, replica_groups=mesh['grp_0'=12,'grp_1'=8,'lane_0'=4,'lane_1'=2] {'lane_0'}, dimensions={0} | all-to-all | bytes 131072 | tf_op jit(solution)/shard_map/all_to_all | solution.py:23
  23.1 1.4 %shard_map.78.counts_ref = bf16[4,192,1024]{2,1,0:T(8,128)(2,1)S(1)} custom-call(bf16[4,2,4,8,128]{4,3,2,1,0:T(8,128)(2,1)S(1)} %all_to_all.25.marks_ref), custom_call_target="tpu_custom_call" | custom-call | flops 6291456 | bytes 1638400 | tf_op jit(solution)/shard_map/pallas_call | solution.py:41
  24.5 0.0 copy-start.3
  24.5 0.0 collective-permute-done.pair_ref
  24.5 0.6 shard_map.79
  25.1 0.0 copy-start.2
  25.1 9.4 %all_to_all.26 = bf16[4,192,256]{2,1,0:T(8,128)(2,1)S(1)} all-to-all(bf16[4,192,256]{2,1,0:T(8,128)(2,1)S(1)} %shard_map.79), channel_id=1, replica_groups=mesh['grp_0'=12,'grp_1'=8,'lane_0'=4,'lane_1'=2] {'lane_0'}, dimensions={0} | all-to-all | bytes 786432 | tf_op jit(solution)/shard_map/all_to_all | solution.py:23
  34.6 0.1 reduce_sum.48
  34.6 0.0 copy-start.1
  34.6 0.7 reshape.36
  35.3 13.6 %all-to-all-start.2 = ((bf16[96,2,256]{2,1,0:T(2,128)(2,1)}), bf16[96,2,256]{2,1,0:T(2,128)(2,1)S(1)}, u32[]{:S(2)}, u32[]{:S(2)}) async-start(bf16[96,2,256]{2,1,0:T(2,128)(2,1)} %reshape.36), calls=%async_computation.2 | async-start | bytes 196608 | tf_op jit(solution)/shard_map/all_to_all | solution.py:23
  48.9 0.0 copy-done.3
  48.9 0.1 copy.13
  49.0 0.1 eq.16
  49.2 13.3 %all-to-all-done.2 = bf16[96,2,256]{2,1,0:T(2,128)(2,1)S(1)} async-done(((bf16[96,2,256]{2,1,0:T(2,128)(2,1)}), bf16[96,2,256]{2,1,0:T(2,128)(2,1)S(1)}, u32[]{:S(2)}, u32[]{:S(2)}) %all-to-all-start.2) | async-done | bytes 98336 | tf_op jit(solution)/shard_map/all_to_all | solution.py:23
  62.5 0.4 multiply_reduce_fusion
  62.9 16.2 %all_to_all.27 = f32[24,1,128]{2,1,0:T(1,128)S(1)} all-to-all(f32[24,1,128]{2,1,0:T(1,128)S(1)} %broadcast_in_dim.4), channel_id=1, replica_groups=mesh['grp_0'=12,'grp_1'=8,'lane_0'=4,'lane_1'=2] {'grp_0','lane_1'}, dimensions={0} | all-to-all | bytes 24576 | tf_op jit(solution)/shard_map/all_to_all | solution.py:23
  79.2 11.6 %all_to_all.28 = f32[32,1,128]{2,1,0:T(1,128)S(1)} all-to-all(f32[32,1,128]{2,1,0:T(1,128)S(1)} %broadcast_in_dim.5), channel_id=1, replica_groups=mesh['grp_0'=12,'grp_1'=8,'lane_0'=4,'lane_1'=2] {'grp_1','lane_0'}, dimensions={0} | all-to-all | bytes 32768 | tf_op jit(solution)/shard_map/all_to_all | solution.py:23
  90.8 0.6 reduce_sum.52
  92.1 0.0 copy-done.2
  92.2 0.6 sqrt_add_fusion
  92.7 0.1 broadcast_multiply_fusion
  92.8 0.0 copy-done.1
  92.8 1.2 %divide_subtract_fusion = f32[4,256,256]{2,1,0:T(8,128)} fusion(f32[4,256,256]{2,1,0:T(8,128)S(1)} %copy-done.1, f32[4,256,256]{2,1,0:T(8,128)S(1)} %bitcast.12, f32[4,256]{1,0:T(4,128)S(1)} %get-tuple-element.2), kind=kLoop, calls=%fused_computation.2 | loop fusion | flops 524288 | bytes 3149824 | tf_op jit(solution)/shard_map/sub | solution.py:155
  (8 shorter events, 0.1 us)
Async XLA Ops:
  1.4 14.9 %copy-start = (s32[1024,4,8]{0,2,1:T(8,128)S(1)}, s32[1024,4,8]{0,2,1:T(8,128)}, u32[]{:S(2)}) copy-start(s32[1024,4,8]{0,2,1:T(8,128)} %param.8) | copy-start | bytes 393220
  3.8 20.7 %collective-permute-start = (bf16[32,128,256]{2,1,0:T(8,128)(2,1)S(1)}, bf16[32,128,256]{2,1,0:T(8,128)(2,1)S(1)}, u32[]{:S(2)}, u32[]{:S(2)}) collective-permute-start(bf16[32,128,256]{2,1,0:T(8,128)(2,1)S(1)} %fusion.own_ref), channel_id=1, source_target_pairs={{0,1},{1,0},{2,3},{3,2},{4,5},{5,4},{6,7},{7,6},{8,9},{9,8},{10,11... | collective-permute-start | bytes 6291464 | tf_op jit(solution)/shard_map/ppermute | solution.py:123
  24.5 24.4 %copy-start.3 = (s32[1,1,96,2]{2,3,1,0:T(2,128)S(1)}, s32[1,1,96,2]{2,3,1,0:T(2,128)}, u32[]{:S(2)}) copy-start(s32[1,1,96,2]{2,3,1,0:T(2,128)} %param.9) | copy-start | bytes 2308
  25.1 67.0 %copy-start.2 = (f32[4,256]{1,0:T(4,128)S(1)}, f32[4,256]{1,0:T(4,128)}, u32[]{:S(2)}) copy-start(f32[4,256]{1,0:T(4,128)} %param.11) | copy-start | bytes 12292
  34.6 58.2 %copy-start.1 = (f32[4,256,256]{2,1,0:T(8,128)S(1)}, f32[4,256,256]{2,1,0:T(8,128)}, u32[]{:S(2)}) copy-start(f32[4,256,256]{2,1,0:T(8,128)} %param.10) | copy-start | bytes 3145732
  35.3 27.1 %all-to-all-start.2 = ((bf16[96,2,256]{2,1,0:T(2,128)(2,1)}), bf16[96,2,256]{2,1,0:T(2,128)(2,1)S(1)}, u32[]{:S(2)}, u32[]{:S(2)}) async-start(bf16[96,2,256]{2,1,0:T(2,128)(2,1)} %reshape.36), calls=%async_computation.2 | async-start | bytes 196608 | tf_op jit(solution)/shard_map/all_to_all | solution.py:23

commit v3 on v2

--- a/solution.py
+++ b/solution.py
@@ -1,3 +1,4 @@
+import functools
 import math
 
 import jax
@@ -28,21 +29,21 @@
     return exchange(jnp.broadcast_to(x.reshape(1, 1, 128), (count, 1, 128)), axes)
 
 
-def sum_over_all(row):
+def parts_of_sum(row):
     row = jnp.sum(gathered(row, ("grp_0", "lane_1")), axis=0)
-    return jnp.sum(gathered(row, ("grp_1", "lane_0")))
+    return gathered(row, ("grp_1", "lane_0"))
 
 
 VMEM = pl.BlockSpec(memory_space=pltpu.VMEM)
 
 
 def kernel_call(kernel, out_shape, flops, *args):
-    moved = sum(x.size * x.dtype.itemsize for x in (*args, out_shape))
+    moved = sum(x.size * x.dtype.itemsize for x in (*args, *jax.tree.leaves(out_shape)))
     return pl.pallas_call(
         kernel,
         out_shape=out_shape,
         in_specs=[VMEM] * len(args),
-        out_specs=VMEM,
+        out_specs=jax.tree.map(lambda _: VMEM, out_shape),
         compiler_params=pltpu.CompilerParams(vmem_limit_bytes=16 * 1024 * 1024),
         cost_estimate=pl.CostEstimate(flops=flops, bytes_accessed=moved, transcendentals=0),
     )(*args)
@@ -76,29 +77,51 @@
                 out_ref[chip, :, start : start + samples] = total
 
 
-def sums_kernel(counts_ref, own_ref, pair_ref, out_ref):
-    chips, _, terms = counts_ref.shape
-    cores = lax.axis_size("lane_1")
-    tables = own_ref.shape[0] // (chips * cores)
-    width = own_ref.shape[2]
+def other_half_kernel(scaled_ref, out_ref):
+    chips, tables = out_ref.shape[:2]
+    other = 1 - lax.axis_index("lane_1")
+    for chip in range(chips):
+        out_ref[chip] = scaled_ref[pl.ds((2 * chip + other) * tables, tables)]
+
+
+def products(counts_ref, chip, core, values):
+    tables, samples, width = values.shape
+    start = pl.multiple_of(core * (tables * samples), tables * samples)
+    return jnp.dot(
+        counts_ref[chip, :, pl.ds(start, tables * samples)],
+        values.reshape(tables * samples, width),
+        preferred_element_type=jnp.float32,
+    )
+
+
+def own_kernel(counts_ref, scaled_ref, out_ref):
     core = lax.axis_index("lane_1")
-    half = terms // cores
-    for chip in range(chips):
-        start = (chip * cores + core) * tables
-        mine = pl.multiple_of(core * half, half)
-        other = pl.multiple_of((1 - core) * half, half)
-        out_ref[chip] = (
-            jnp.dot(
-                counts_ref[chip, :, pl.ds(mine, half)],
-                own_ref[pl.ds(start, tables)].reshape(half, width),
-                preferred_element_type=jnp.float32,
-            )
-            + jnp.dot(
-                counts_ref[chip, :, pl.ds(other, half)],
-                pair_ref[pl.ds(start, tables)].reshape(half, width),
-                preferred_element_type=jnp.float32,
-            )
-        ).astype(out_ref.dtype)
+    chips = counts_ref.shape[0]
+    tables = scaled_ref.shape[0] // (2 * chips)
+    for chip in range(chips):
+        values = scaled_ref[pl.ds((2 * chip + core) * tables, tables)]
+        out_ref[chip] = products(counts_ref, chip, core, values)
+
+
+def pair_kernel(counts_ref, pair_ref, own_ref, out_ref):
+    core = lax.axis_index("lane_1")
+    for chip in range(counts_ref.shape[0]):
+        both = own_ref[chip] + products(counts_ref, chip, 1 - core, pair_ref[chip])
+        out_ref[chip] = both.astype(out_ref.dtype)
+
+
+def update_kernel(scale, limit, norms_ref, square_ref, rows_ref, weights_ref, accum_ref, new_weights_ref, new_accum_ref):
+    tables, _, _ = weights_ref.shape
+    total = scale * jnp.sum(jnp.sum(norms_ref[...], axis=0), axis=(0, 1), keepdims=True)
+    clip = limit / jnp.maximum(jnp.sqrt(total), limit)
+    new_accum = accum_ref[...] + clip * clip * square_ref[...]
+    new_accum_ref[...] = new_accum
+    step = (LEARN_RATE * clip) / (jnp.sqrt(new_accum) + EPSILON)
+    columns = jnp.transpose(jnp.concatenate([step, step], axis=0))
+    for table in range(tables):
+        new_weights_ref[table] = (
+            weights_ref[table] - columns[:, table : table + 1] * rows_ref[table]
+        )
 
 
 def per_device(grad_pooled, bag_len, lookup_slot, slot_row, weights, accum):
@@ -116,11 +139,11 @@
         lookup_slot.transpose(1, 2, 0),
     )
     marks = exchange(marks, "lane_0")
-    scaled = (
-        grad_pooled.astype(jnp.float32) * (1.0 / bag_len.astype(jnp.float32))[:, :, None]
-    ).astype(jnp.bfloat16)
+    scaled = (grad_pooled.astype(jnp.float32) * (1.0 / bag_len.astype(jnp.float32))[:, :, None]).astype(jnp.bfloat16)
     scaled = scaled.transpose(1, 0, 2)
-    pair = lax.ppermute(scaled, "lane_1", [(0, 1), (1, 0)])
+    half = jax.ShapeDtypeStruct((chips, tables_here, batch_rows, embed_width), jnp.bfloat16)
+    pair = kernel_call(other_half_kernel, half, half.size, scaled)
+    pair = lax.ppermute(pair, "lane_1", [(0, 1), (1, 0)])
     terms = cores * tables_here * batch_rows
     counts = kernel_call(
         counts_kernel,
@@ -128,32 +151,37 @@
         chips * number_slots * terms * bag_depth,
         marks,
     )
-    partial_value = kernel_call(
-        sums_kernel,
-        jax.ShapeDtypeStruct((chips, number_slots, embed_width), jnp.bfloat16),
-        2 * chips * number_slots * terms * embed_width,
-        counts,
-        scaled,
-        pair,
-    )
+    flops = chips * number_slots * terms * embed_width
+    part_shape = (chips, number_slots, embed_width)
+    own = kernel_call(own_kernel, jax.ShapeDtypeStruct(part_shape, jnp.float32), flops, counts, scaled)
+    own, targets = lax.optimization_barrier((own, slot_row.reshape(1, number_slots)))
+    partial_value = kernel_call(pair_kernel, jax.ShapeDtypeStruct(part_shape, jnp.bfloat16), flops, counts, pair, own)
     partial_value = exchange(partial_value, "lane_0")
     slot_sum = jnp.sum(partial_value.astype(jnp.float32), axis=0).astype(jnp.bfloat16)
     outgoing = slot_sum.reshape(group_count, SLOTS_PEER, embed_width)
     incoming = exchange(outgoing, GRP).reshape(number_slots, embed_width)
-    targets = slot_row.reshape(1, number_slots)
     local_rows = accum.shape[0] * accum.shape[1]
     row_ids = lax.broadcasted_iota(jnp.int32, (local_rows, 1), 0)
     placing = (row_ids == targets).astype(jnp.bfloat16)
     row_grad = jnp.dot(placing, incoming, preferred_element_type=jnp.float32)
     square_mean = jnp.mean(row_grad * row_grad, axis=1)
     norm_row = jnp.sum(square_mean.reshape(-1, 128), axis=0)
-    norm_total = embed_width * sum_over_all(norm_row)
+    norm_row, square_mean = lax.optimization_barrier((norm_row, square_mean.reshape(accum.shape)))
+    norms = parts_of_sum(norm_row)
     clip_limit = 0.5 * math.sqrt(group_count * lane_count * number_slots * embed_width)
-    clip_factor = clip_limit / jnp.maximum(jnp.sqrt(norm_total), clip_limit)
-    new_accum = accum + clip_factor * clip_factor * square_mean.reshape(accum.shape)
-    step_rows = LEARN_RATE * clip_factor * row_grad.reshape(weights.shape)
-    new_weights = weights - step_rows / (jnp.sqrt(new_accum)[:, :, None] + EPSILON)
-    return (new_weights, new_accum)
+    return kernel_call(
+        functools.partial(update_kernel, embed_width, clip_limit),
+        (
+            jax.ShapeDtypeStruct(weights.shape, jnp.float32),
+            jax.ShapeDtypeStruct(accum.shape, jnp.float32),
+        ),
+        2 * weights.size,
+        norms,
+        square_mean,
+        row_grad.reshape(weights.shape),
+        weights,
+        accum,
+    )
 
 
 def solution(mesh):

time: 94.5 us -> 94.3 us (level)
  blocking collectives: 44.1 us -> 63.6 us
  starting transfers between devices: 26 us -> 15.7 us
  waiting for transfers between devices: 13.3 us -> 4.21 us
  Pallas kernels: 1.99 us -> 5.54 us
  other arithmetic: 5.77 us -> 3.26 us
    all_to_all x4, blocking collectives: 44.1 us -> 63.6 us  [exchange(): return lax.all_to_all(x, axes, split_axis=0, concat_axis=0, tiled=True)]
    all_to_all x1, starting transfers between devices: 13.6 us -> 3.28 us  [exchange(): return lax.all_to_all(x, axes, split_axis=0, concat_axis=0, tiled=True)]
    all_to_all x1, waiting for transfers between devices: 13.3 us -> 4.2 us  [exchange(): return lax.all_to_all(x, axes, split_axis=0, concat_axis=0, tiled=True)]
    pallas_call x3 -> x6, Pallas kernels: 1.99 us -> 5.54 us  [kernel_call(): pl.pallas_call(kernel, out_shape=out_shape, in_specs=[VMEM] * len(args),...]
    sub x1 -> x0, other arithmetic: 1.2 us -> none  [per_device(): weights - step_rows / (jnp.sqrt(new_accum)[:, :, None] + EPSILON)]
  transfers between devices with their start and end apart: 2 -> 2, of which waited for: 1 -> 1; matrix products, arithmetic and copies ran while one was open for 0% -> 0% of each run, Pallas kernels for 1% -> 3%
where the time goes in v3:
time: 94.3 us; the launch traced here: 93.8 us
  blocking collectives  63.6 us (67%)
  starting transfers between devices  15.7 us (17%)
  Pallas kernels  5.54 us (6%)
  waiting for transfers between devices  4.21 us (4%)
  other arithmetic  3.26 us (3%)
    all_to_all x4, blocking collectives, exchange(): return lax.all_to_all(x, axes, split_axis=0, concat_axis=0, tiled=True)  63.6 us
    ppermute x1, starting transfers between devices, per_device(): pair = lax.ppermute(pair, 'lane_1', [(0, 1), (1, 0)])  12.4 us
    pallas_call x6, Pallas kernels, kernel_call(): pl.pallas_call(kernel, out_shape=out_shape, in_specs=[VMEM] * len(args),...  5.54 us
    all_to_all x1, waiting for transfers between devices, exchange(): return lax.all_to_all(x, axes, split_axis=0, concat_axis=0, tiled=True)  4.2 us
    all_to_all x1, starting transfers between devices, exchange(): return lax.all_to_all(x, axes, split_axis=0, concat_axis=0, tiled=True)  3.28 us
    transpose x1, other arithmetic, per_device(): scaled = scaled.transpose(1, 0, 2)  2.43 us
  transfers between devices with their start and end apart: 2, of which 1 were waited for; matrix products, arithmetic and copies ran while one was open for 0% of the time, Pallas kernels for 3%

profile of v3, /device:TPU:1, one launch (start us, length us, event | category | flops | bytes accessed | tf_op | source)
XLA Modules:
  0.0 93.8 jit_solution(16448394094369679625)
XLA Ops:
  0.6 0.7 convert_divide_fusion
  1.4 2.4 %fusion.scaled_ref = bf16[32,128,256]{2,1,0:T(8,128)(2,1)S(1)} fusion(bf16[128,32,256]{2,1,0:T(8,128)(2,1)} %param.6, f32[128,32]{0,1:T(8,128)S(1)} %convert_divide_fusion), kind=kLoop, calls=%fused_computation.1 | loop fusion | flops 3145728 | bytes 4210688 | tf_op jit(solution)/shard_map/transpose | solution.py:143
  3.8 0.0 copy-start.1
  3.8 0.0 copy-start.3
  3.8 0.1 shard_map.80
  3.9 12.4 %collective-permute-start = (bf16[4,4,128,256]{3,2,1,0:T(8,128)(2,1)S(1)}, bf16[4,4,128,256]{3,2,1,0:T(8,128)(2,1)}, u32[]{:S(2)}, u32[]{:S(2)}) collective-permute-start(bf16[4,4,128,256]{3,2,1,0:T(8,128)(2,1)S(1)} %shard_map.80), channel_id=1, source_target_pairs={{0,1},{1,0},{2,3},{3,2},{4,5},{5,4},{6,7},{7,6},{8,9},{9,8},{10,11... | collective-permute-start | bytes 3145736 | tf_op jit(solution)/shard_map/ppermute | solution.py:146
  16.3 0.0 copy-done.1
  16.3 0.6 shard_map.77
  16.9 3.3 %all-to-all-start = ((bf16[4,2,4,8,128]{4,3,2,1,0:T(8,128)(2,1)}), bf16[4,2,4,8,128]{4,3,2,1,0:T(8,128)(2,1)S(1)}, u32[]{:S(2)}, u32[]{:S(2)}) async-start(bf16[4,2,4,8,128]{4,3,2,1,0:T(8,128)(2,1)} %shard_map.77), calls=%async_computation | async-start | bytes 131072 | tf_op jit(solution)/shard_map/all_to_all | solution.py:24
  20.2 0.0 copy-done.3
  20.2 0.1 copy.14
  20.4 0.1 reshape.35
  20.5 4.2 %all-to-all-done.marks_ref = bf16[4,2,4,8,128]{4,3,2,1,0:T(8,128)(2,1)S(1)} async-done(((bf16[4,2,4,8,128]{4,3,2,1,0:T(8,128)(2,1)}), bf16[4,2,4,8,128]{4,3,2,1,0:T(8,128)(2,1)S(1)}, u32[]{:S(2)}, u32[]{:S(2)}) %all-to-all-start) | async-done | bytes 65568 | tf_op jit(solution)/shard_map/all_to_all | solution.py:24
  24.7 1.4 %shard_map.78.counts_ref = bf16[4,192,1024]{2,1,0:T(8,128)(2,1)S(1)} custom-call(bf16[4,2,4,8,128]{4,3,2,1,0:T(8,128)(2,1)S(1)} %all-to-all-done.marks_ref), custom_call_target="tpu_custom_call" | custom-call | flops 6291456 | bytes 1638400 | tf_op jit(solution)/shard_map/pallas_call | solution.py:42
  26.1 0.4 shard_map.79.own_ref
  26.5 0.0 collective-permute-done.pair_ref
  26.5 1.6 %shard_map.81 = bf16[4,192,256]{2,1,0:T(8,128)(2,1)S(1)} custom-call(bf16[4,192,1024]{2,1,0:T(8,128)(2,1)S(1)} %shard_map.78.counts_ref, bf16[4,4,128,256]{3,2,1,0:T(8,128)(2,1)} %collective-permute-done.pair_ref, f32[4,192,256]{2,1,0:T(8,128)S(1)} %shard_map.79.own_ref), custom_call_target="tpu_custom_call" | custom-call | flops 201326592 | bytes 3801088 | tf_op jit(solution)/shard_map/pallas_call | solution.py:42
  28.1 0.0 copy-start
  28.1 0.0 copy-start.2
  28.1 9.5 %all_to_all.25 = bf16[4,192,256]{2,1,0:T(8,128)(2,1)S(1)} all-to-all(bf16[4,192,256]{2,1,0:T(8,128)(2,1)S(1)} %shard_map.81), channel_id=1, replica_groups=mesh['grp_0'=12,'grp_1'=8,'lane_0'=4,'lane_1'=2] {'lane_0'}, dimensions={0} | all-to-all | bytes 786432 | tf_op jit(solution)/shard_map/all_to_all | solution.py:24
  37.6 0.1 reduce_sum.39
  37.7 26.3 %all_to_all.26 = bf16[96,2,256]{2,1,0:T(2,128)(2,1)S(1)} all-to-all(bf16[96,2,256]{2,1,0:T(2,128)(2,1)S(1)} %reshape.36), channel_id=1, replica_groups=mesh['grp_0'=12,'grp_1'=8,'lane_0'=4,'lane_1'=2] {'grp_0','grp_1'}, dimensions={0} | all-to-all | bytes 196608 | tf_op jit(solution)/shard_map/all_to_all | solution.py:24
  64.0 0.4 multiply_reduce_fusion
  64.5 16.1 %all_to_all.27 = f32[24,1,128]{2,1,0:T(1,128)S(1)} all-to-all(f32[24,1,128]{2,1,0:T(1,128)S(1)} %broadcast_in_dim.4), channel_id=1, replica_groups=mesh['grp_0'=12,'grp_1'=8,'lane_0'=4,'lane_1'=2] {'grp_0','lane_1'}, dimensions={0} | all-to-all | bytes 24576 | tf_op jit(solution)/shard_map/all_to_all | solution.py:24
  80.7 11.7 %all_to_all.28.norms_ref = f32[32,1,128]{2,1,0:T(1,128)S(1)} all-to-all(f32[32,1,128]{2,1,0:T(1,128)S(1)} %broadcast_in_dim.5), channel_id=1, replica_groups=mesh['grp_0'=12,'grp_1'=8,'lane_0'=4,'lane_1'=2] {'grp_1','lane_0'}, dimensions={0} | all-to-all | bytes 32768 | tf_op jit(solution)/shard_map/all_to_all | solution.py:24
  92.3 0.0 copy-done
  92.3 0.0 copy-done.2
  92.3 1.5 %shard_map.82 = (f32[4,256,256]{2,1,0:T(8,128)}, f32[4,256]{1,0:T(4,128)}) custom-call(f32[32,1,128]{2,1,0:T(1,128)S(1)} %all_to_all.28.norms_ref, f32[4,256]{1,0:T(4,128)S(1)} %div.21.square_ref, f32[4,256,256]{2,1,0:T(8,128)S(1)} %bitcast.11, f32[4,256,256]{2,1,0:T(8,128)S(1)} %copy-done, f32[4,256]{1,0:T(4,128)S(1)} %copy-done.2), custom_call_target="tpu_custom_call" | custom-call | flops 524288 | bytes 3174400 | tf_op jit(solution)/shard_map/pallas_call | solution.py:42
  (8 shorter events, 0.2 us)
Async XLA Ops:
  3.8 12.5 %copy-start.1 = (s32[1024,4,8]{0,2,1:T(8,128)S(1)}, s32[1024,4,8]{0,2,1:T(8,128)}, u32[]{:S(2)}) copy-start(s32[1024,4,8]{0,2,1:T(8,128)} %param.8) | copy-start | bytes 393220
  3.8 16.4 %copy-start.3 = (s32[1,1,96,2]{2,3,1,0:T(2,128)S(1)}, s32[1,1,96,2]{2,3,1,0:T(2,128)}, u32[]{:S(2)}) copy-start(s32[1,1,96,2]{2,3,1,0:T(2,128)} %param.9) | copy-start | bytes 2308
  3.9 22.6 %collective-permute-start = (bf16[4,4,128,256]{3,2,1,0:T(8,128)(2,1)S(1)}, bf16[4,4,128,256]{3,2,1,0:T(8,128)(2,1)}, u32[]{:S(2)}, u32[]{:S(2)}) collective-permute-start(bf16[4,4,128,256]{3,2,1,0:T(8,128)(2,1)S(1)} %shard_map.80), channel_id=1, source_target_pairs={{0,1},{1,0},{2,3},{3,2},{4,5},{5,4},{6,7},{7,6},{8,9},{9,8},{10,11... | collective-permute-start | bytes 3145736 | tf_op jit(solution)/shard_map/ppermute | solution.py:146
  16.9 7.7 %all-to-all-start = ((bf16[4,2,4,8,128]{4,3,2,1,0:T(8,128)(2,1)}), bf16[4,2,4,8,128]{4,3,2,1,0:T(8,128)(2,1)S(1)}, u32[]{:S(2)}, u32[]{:S(2)}) async-start(bf16[4,2,4,8,128]{4,3,2,1,0:T(8,128)(2,1)} %shard_map.77), calls=%async_computation | async-start | bytes 131072 | tf_op jit(solution)/shard_map/all_to_all | solution.py:24
  28.1 64.3 %copy-start = (f32[4,256,256]{2,1,0:T(8,128)S(1)}, f32[4,256,256]{2,1,0:T(8,128)}, u32[]{:S(2)}) copy-start(f32[4,256,256]{2,1,0:T(8,128)} %weights_ref.1) | copy-start | bytes 3145732
  28.1 64.2 %copy-start.2 = (f32[4,256]{1,0:T(4,128)S(1)}, f32[4,256]{1,0:T(4,128)}, u32[]{:S(2)}) copy-start(f32[4,256]{1,0:T(4,128)} %accum_ref.1) | copy-start | bytes 12292

commit v4 on v3

--- a/solution.py
+++ b/solution.py
@@ -37,19 +37,36 @@
 VMEM = pl.BlockSpec(memory_space=pltpu.VMEM)
 
 
-def kernel_call(kernel, out_shape, flops, *args):
-    moved = sum(x.size * x.dtype.itemsize for x in (*args, *jax.tree.leaves(out_shape)))
+HBM = pl.BlockSpec(memory_space=pltpu.MemorySpace.HBM)
+
+
+def kernel_call(kernel, out_shape, flops, *args, far_in=(), far_out=(), scratch=()):
+    outs = jax.tree.leaves(out_shape)
+    args = [
+        pltpu.with_memory_space_constraint(x, pltpu.MemorySpace.HBM) if index in far_in else x
+        for index, x in enumerate(args)
+    ]
+    moved = sum(x.size * x.dtype.itemsize for x in (*args, *outs))
+    out_specs = [HBM if index in far_out else VMEM for index in range(len(outs))]
     return pl.pallas_call(
         kernel,
         out_shape=out_shape,
-        in_specs=[VMEM] * len(args),
-        out_specs=jax.tree.map(lambda _: VMEM, out_shape),
+        in_specs=[HBM if index in far_in else VMEM for index in range(len(args))],
+        out_specs=tuple(out_specs) if isinstance(out_shape, tuple) else out_specs[0],
+        scratch_shapes=list(scratch),
         compiler_params=pltpu.CompilerParams(vmem_limit_bytes=16 * 1024 * 1024),
         cost_estimate=pl.CostEstimate(flops=flops, bytes_accessed=moved, transcendentals=0),
     )(*args)
 
 
-def marks_kernel(slot_ref, out_ref):
+def marks_kernel(far_slot_ref, far_length_ref, out_ref, share_ref, slot_ref, length_ref, arrived):
+    lengths = pltpu.make_async_copy(far_length_ref, length_ref, arrived.at[0])
+    slots = pltpu.make_async_copy(far_slot_ref, slot_ref, arrived.at[1])
+    lengths.start()
+    slots.start()
+    lengths.wait()
+    share_ref[...] = 1.0 / length_ref[...].astype(jnp.float32)
+    slots.wait()
     chips, cores, tables, _, samples = out_ref.shape
     for chip in range(chips):
         for core in range(cores):
@@ -103,25 +120,39 @@
         out_ref[chip] = products(counts_ref, chip, core, values)
 
 
-def pair_kernel(counts_ref, pair_ref, own_ref, out_ref):
+def pair_kernel(counts_ref, own_ref, pair_ref, out_ref, held, arrived):
     core = lax.axis_index("lane_1")
-    for chip in range(counts_ref.shape[0]):
-        both = own_ref[chip] + products(counts_ref, chip, 1 - core, pair_ref[chip])
+    chips = counts_ref.shape[0]
+    copies = [
+        pltpu.make_async_copy(pair_ref.at[chip], held.at[chip], arrived.at[chip]) for chip in range(chips)
+    ]
+    for copy in copies:
+        copy.start()
+    for chip in range(chips):
+        copies[chip].wait()
+        both = own_ref[chip] + products(counts_ref, chip, 1 - core, held[chip])
         out_ref[chip] = both.astype(out_ref.dtype)
 
 
-def update_kernel(scale, limit, norms_ref, square_ref, rows_ref, weights_ref, accum_ref, new_weights_ref, new_accum_ref):
-    tables, _, _ = weights_ref.shape
+def update_kernel(
+    scale, limit, norms_ref, square_ref, rows_ref, weights_ref, accum_ref, new_weights_ref, new_accum_ref, done, sent
+):
+    tables = weights_ref.shape[0]
     total = scale * jnp.sum(jnp.sum(norms_ref[...], axis=0), axis=(0, 1), keepdims=True)
     clip = limit / jnp.maximum(jnp.sqrt(total), limit)
     new_accum = accum_ref[...] + clip * clip * square_ref[...]
-    new_accum_ref[...] = new_accum
     step = (LEARN_RATE * clip) / (jnp.sqrt(new_accum) + EPSILON)
     columns = jnp.transpose(jnp.concatenate([step, step], axis=0))
+    copies = [
+        pltpu.make_async_copy(done.at[table], new_weights_ref.at[table], sent.at[table])
+        for table in range(tables)
+    ]
     for table in range(tables):
-        new_weights_ref[table] = (
-            weights_ref[table] - columns[:, table : table + 1] * rows_ref[table]
-        )
+        done[table] = weights_ref[table] - columns[:, table : table + 1] * rows_ref[table]
+        copies[table].start()
+    new_accum_ref[...] = new_accum
+    for copy in copies:
+        copy.wait()
 
 
 def per_device(grad_pooled, bag_len, lookup_slot, slot_row, weights, accum):
@@ -132,14 +163,24 @@
     batch_rows, table_count, embed_width = grad_pooled.shape
     tables_here = table_count // lane_count
     bag_depth = lookup_slot.shape[2]
-    marks = kernel_call(
+    marks, share = kernel_call(
         marks_kernel,
-        jax.ShapeDtypeStruct((chips, cores, tables_here, bag_depth, batch_rows), jnp.bfloat16),
+        (
+            jax.ShapeDtypeStruct((chips, cores, tables_here, bag_depth, batch_rows), jnp.bfloat16),
+            jax.ShapeDtypeStruct((table_count, batch_rows), jnp.float32),
+        ),
         lookup_slot.size,
         lookup_slot.transpose(1, 2, 0),
+        bag_len.transpose(1, 0),
+        far_in=(0, 1),
+        scratch=(
+            pltpu.VMEM((tables_here, bag_depth, chips * cores * batch_rows), jnp.int32),
+            pltpu.VMEM((table_count, batch_rows), jnp.int32),
+            pltpu.SemaphoreType.DMA((2,)),
+        ),
     )
     marks = exchange(marks, "lane_0")
-    scaled = (grad_pooled.astype(jnp.float32) * (1.0 / bag_len.astype(jnp.float32))[:, :, None]).astype(jnp.bfloat16)
+    scaled = (grad_pooled.astype(jnp.float32) * share.transpose(1, 0)[:, :, None]).astype(jnp.bfloat16)
     scaled = scaled.transpose(1, 0, 2)
     half = jax.ShapeDtypeStruct((chips, tables_here, batch_rows, embed_width), jnp.bfloat16)
     pair = kernel_call(other_half_kernel, half, half.size, scaled)
@@ -155,7 +196,16 @@
     part_shape = (chips, number_slots, embed_width)
     own = kernel_call(own_kernel, jax.ShapeDtypeStruct(part_shape, jnp.float32), flops, counts, scaled)
     own, targets = lax.optimization_barrier((own, slot_row.reshape(1, number_slots)))
-    partial_value = kernel_call(pair_kernel, jax.ShapeDtypeStruct(part_shape, jnp.bfloat16), flops, counts, pair, own)
+    partial_value = kernel_call(
+        pair_kernel,
+        jax.ShapeDtypeStruct(part_shape, jnp.bfloat16),
+        flops,
+        counts,
+        own,
+        pair,
+        far_in=(2,),
+        scratch=(pltpu.VMEM(half.shape, half.dtype), pltpu.SemaphoreType.DMA((chips,))),
+    )
     partial_value = exchange(partial_value, "lane_0")
     slot_sum = jnp.sum(partial_value.astype(jnp.float32), axis=0).astype(jnp.bfloat16)
     outgoing = slot_sum.reshape(group_count, SLOTS_PEER, embed_width)
@@ -181,6 +231,8 @@
         row_grad.reshape(weights.shape),
         weights,
         accum,
+        far_out=(0,),
+        scratch=(pltpu.VMEM(weights.shape, weights.dtype), pltpu.SemaphoreType.DMA((tables_here,))),
     )
 
 

time: 94.3 us -> 95.6 us (1.014)
  Pallas kernels: 5.54 us -> 7.53 us
    pallas_call x6, Pallas kernels: 5.54 us -> 7.53 us  [kernel_call(): pl.pallas_call(kernel, out_shape=out_shape, in_specs=[HBM if index in far...]
  transfers between devices with their start and end apart: 2 -> 2, of which waited for: 1 -> 1; matrix products, arithmetic and copies ran while one was open for 0% -> 0% of each run, Pallas kernels for 3% -> 2%
where the time goes in v4:
time: 95.6 us; the launch traced here: 95.1 us
  blocking collectives  63.6 us (67%)
  starting transfers between devices  15.7 us (16%)
  Pallas kernels  7.53 us (8%)
  waiting for transfers between devices  4.21 us (4%)
  other arithmetic  2.55 us (3%)
    all_to_all x4, blocking collectives, exchange(): return lax.all_to_all(x, axes, split_axis=0, concat_axis=0, tiled=True)  63.6 us
    ppermute x1, starting transfers between devices, per_device(): pair = lax.ppermute(pair, 'lane_1', [(0, 1), (1, 0)])  12.4 us
    pallas_call x6, Pallas kernels, kernel_call(): pl.pallas_call(kernel, out_shape=out_shape, in_specs=[HBM if index in far...  7.53 us
    all_to_all x1, waiting for transfers between devices, exchange(): return lax.all_to_all(x, axes, split_axis=0, concat_axis=0, tiled=True)  4.2 us
    all_to_all x1, starting transfers between devices, exchange(): return lax.all_to_all(x, axes, split_axis=0, concat_axis=0, tiled=True)  3.3 us
    transpose x1, other arithmetic, per_device(): scaled = scaled.transpose(1, 0, 2)  2.45 us
  transfers between devices with their start and end apart: 2, of which 1 were waited for; matrix products, arithmetic and copies ran while one was open for 0% of the time, Pallas kernels for 2%

profile of v4, /device:TPU:1, one launch (start us, length us, event | category | flops | bytes accessed | tf_op | source)
XLA Modules:
  0.0 95.1 jit_solution(18291159710376684434)
XLA Ops:
  0.6 1.6 %shard_map.77 = (bf16[4,2,4,8,128]{4,3,2,1,0:T(8,128)(2,1)}, f32[32,128]{1,0:T(8,128)S(1)}) custom-call(s32[4,8,1024]{2,1,0:T(8,128)} %bitcast.15, s32[32,128]{1,0:T(8,128)} %bitcast.17), custom_call_target="tpu_custom_call" | custom-call | flops 32768 | bytes 229376 | tf_op jit(solution)/shard_map/pallas_call | solution.py:51
  2.2 2.4 %fusion.scaled_ref = bf16[32,128,256]{2,1,0:T(8,128)(2,1)S(1)} fusion(bf16[128,32,256]{2,1,0:T(8,128)(2,1)} %param.6, f32[128,32]{0,1:T(8,128)S(1)} %bitcast.14), kind=kLoop, calls=%fused_computation.1 | loop fusion | flops 3145728 | bytes 4210688 | tf_op jit(solution)/shard_map/transpose | solution.py:184
  4.7 0.0 copy-start.2
  4.7 0.1 shard_map.80
  4.8 12.4 %collective-permute-start = (bf16[4,4,128,256]{3,2,1,0:T(8,128)(2,1)S(1)}, bf16[4,4,128,256]{3,2,1,0:T(8,128)(2,1)}, u32[]{:S(2)}, u32[]{:S(2)}) collective-permute-start(bf16[4,4,128,256]{3,2,1,0:T(8,128)(2,1)S(1)} %shard_map.80), channel_id=1, source_target_pairs={{0,1},{1,0},{2,3},{3,2},{4,5},{5,4},{6,7},{7,6},{8,9},{9,8},{10,11... | collective-permute-start | bytes 3145736 | tf_op jit(solution)/shard_map/ppermute | solution.py:187
  17.2 3.3 %all-to-all-start = ((bf16[4,2,4,8,128]{4,3,2,1,0:T(8,128)(2,1)}), bf16[4,2,4,8,128]{4,3,2,1,0:T(8,128)(2,1)S(1)}, u32[]{:S(2)}, u32[]{:S(2)}) async-start(bf16[4,2,4,8,128]{4,3,2,1,0:T(8,128)(2,1)} %get-tuple-element.8), calls=%async_computation | async-start | bytes 131072 | tf_op jit(solution)/shard_map/all_to_all | solution.py:24
  20.5 0.0 copy-done.2
  20.5 0.1 copy.14
  20.6 0.1 reshape.35
  20.7 4.2 %all-to-all-done.marks_ref = bf16[4,2,4,8,128]{4,3,2,1,0:T(8,128)(2,1)S(1)} async-done(((bf16[4,2,4,8,128]{4,3,2,1,0:T(8,128)(2,1)}), bf16[4,2,4,8,128]{4,3,2,1,0:T(8,128)(2,1)S(1)}, u32[]{:S(2)}, u32[]{:S(2)}) %all-to-all-start) | async-done | bytes 65568 | tf_op jit(solution)/shard_map/all_to_all | solution.py:24
  24.9 1.4 %shard_map.78.counts_ref = bf16[4,192,1024]{2,1,0:T(8,128)(2,1)S(1)} custom-call(bf16[4,2,4,8,128]{4,3,2,1,0:T(8,128)(2,1)S(1)} %all-to-all-done.marks_ref), custom_call_target="tpu_custom_call" | custom-call | flops 6291456 | bytes 1638400 | tf_op jit(solution)/shard_map/pallas_call | solution.py:51
  26.3 0.4 shard_map.79.own_ref
  26.7 0.0 collective-permute-done.pair_ref
  26.7 2.0 %shard_map.81 = bf16[4,192,256]{2,1,0:T(8,128)(2,1)S(1)} custom-call(bf16[4,192,1024]{2,1,0:T(8,128)(2,1)S(1)} %shard_map.78.counts_ref, f32[4,192,256]{2,1,0:T(8,128)S(1)} %shard_map.79.own_ref, bf16[4,4,128,256]{3,2,1,0:T(8,128)(2,1)} %collective-permute-done.pair_ref), custom_call_target="tpu_custom_call" | custom-call | flops 201326592 | bytes 3801088 | tf_op jit(solution)/shard_map/pallas_call | solution.py:51
  28.7 0.0 copy-start
  28.7 0.0 copy-start.1
  28.7 9.5 %all_to_all.25 = bf16[4,192,256]{2,1,0:T(8,128)(2,1)S(1)} all-to-all(bf16[4,192,256]{2,1,0:T(8,128)(2,1)S(1)} %shard_map.81), channel_id=1, replica_groups=mesh['grp_0'=12,'grp_1'=8,'lane_0'=4,'lane_1'=2] {'lane_0'}, dimensions={0} | all-to-all | bytes 786432 | tf_op jit(solution)/shard_map/all_to_all | solution.py:24
  38.3 0.1 reduce_sum.39
  38.4 26.2 %all_to_all.26 = bf16[96,2,256]{2,1,0:T(2,128)(2,1)S(1)} all-to-all(bf16[96,2,256]{2,1,0:T(2,128)(2,1)S(1)} %reshape.36), channel_id=1, replica_groups=mesh['grp_0'=12,'grp_1'=8,'lane_0'=4,'lane_1'=2] {'grp_0','grp_1'}, dimensions={0} | all-to-all | bytes 196608 | tf_op jit(solution)/shard_map/all_to_all | solution.py:24
  64.7 0.4 multiply_reduce_fusion
  65.1 16.1 %all_to_all.27 = f32[24,1,128]{2,1,0:T(1,128)S(1)} all-to-all(f32[24,1,128]{2,1,0:T(1,128)S(1)} %broadcast_in_dim.4), channel_id=1, replica_groups=mesh['grp_0'=12,'grp_1'=8,'lane_0'=4,'lane_1'=2] {'grp_0','lane_1'}, dimensions={0} | all-to-all | bytes 24576 | tf_op jit(solution)/shard_map/all_to_all | solution.py:24
  81.3 11.7 %all_to_all.28.norms_ref = f32[32,1,128]{2,1,0:T(1,128)S(1)} all-to-all(f32[32,1,128]{2,1,0:T(1,128)S(1)} %broadcast_in_dim.5), channel_id=1, replica_groups=mesh['grp_0'=12,'grp_1'=8,'lane_0'=4,'lane_1'=2] {'grp_1','lane_0'}, dimensions={0} | all-to-all | bytes 32768 | tf_op jit(solution)/shard_map/all_to_all | solution.py:24
  93.0 0.0 copy-done
  93.0 0.0 copy-done.1
  93.0 2.1 %shard_map.82 = (f32[4,256,256]{2,1,0:T(8,128)}, f32[4,256]{1,0:T(4,128)}) custom-call(f32[32,1,128]{2,1,0:T(1,128)S(1)} %all_to_all.28.norms_ref, f32[4,256]{1,0:T(4,128)S(1)} %div.13.square_ref, f32[4,256,256]{2,1,0:T(8,128)S(1)} %bitcast.13, f32[4,256,256]{2,1,0:T(8,128)S(1)} %copy-done, f32[4,256]{1,0:T(4,128)S(1)} %copy-done.1), custom_call_target="tpu_custom_call" | custom-call | flops 524288 | bytes 3174400 | tf_op jit(solution)/shard_map/pallas_call | solution.py:51
  (8 shorter events, 0.2 us)
Async XLA Ops:
  4.7 15.8 %copy-start.2 = (s32[1,1,96,2]{2,3,1,0:T(2,128)S(1)}, s32[1,1,96,2]{2,3,1,0:T(2,128)}, u32[]{:S(2)}) copy-start(s32[1,1,96,2]{2,3,1,0:T(2,128)} %param.9) | copy-start | bytes 2308
  4.8 21.9 %collective-permute-start = (bf16[4,4,128,256]{3,2,1,0:T(8,128)(2,1)S(1)}, bf16[4,4,128,256]{3,2,1,0:T(8,128)(2,1)}, u32[]{:S(2)}, u32[]{:S(2)}) collective-permute-start(bf16[4,4,128,256]{3,2,1,0:T(8,128)(2,1)S(1)} %shard_map.80), channel_id=1, source_target_pairs={{0,1},{1,0},{2,3},{3,2},{4,5},{5,4},{6,7},{7,6},{8,9},{9,8},{10,11... | collective-permute-start | bytes 3145736 | tf_op jit(solution)/shard_map/ppermute | solution.py:187
  17.2 7.8 %all-to-all-start = ((bf16[4,2,4,8,128]{4,3,2,1,0:T(8,128)(2,1)}), bf16[4,2,4,8,128]{4,3,2,1,0:T(8,128)(2,1)S(1)}, u32[]{:S(2)}, u32[]{:S(2)}) async-start(bf16[4,2,4,8,128]{4,3,2,1,0:T(8,128)(2,1)} %get-tuple-element.8), calls=%async_computation | async-start | bytes 131072 | tf_op jit(solution)/shard_map/all_to_all | solution.py:24
  28.7 64.2 %copy-start = (f32[4,256,256]{2,1,0:T(8,128)S(1)}, f32[4,256,256]{2,1,0:T(8,128)}, u32[]{:S(2)}) copy-start(f32[4,256,256]{2,1,0:T(8,128)} %weights_ref.1) | copy-start | bytes 3145732
  28.7 64.2 %copy-start.1 = (f32[4,256]{1,0:T(4,128)S(1)}, f32[4,256]{1,0:T(4,128)}, u32[]{:S(2)}) copy-start(f32[4,256]{1,0:T(4,128)} %accum_ref.1) | copy-start | bytes 12292

commit v5 on v3

--- a/solution.py
+++ b/solution.py
@@ -37,19 +37,35 @@
 VMEM = pl.BlockSpec(memory_space=pltpu.VMEM)
 
 
-def kernel_call(kernel, out_shape, flops, *args):
-    moved = sum(x.size * x.dtype.itemsize for x in (*args, *jax.tree.leaves(out_shape)))
+HBM = pl.BlockSpec(memory_space=pltpu.MemorySpace.HBM)
+
+
+def kernel_call(kernel, out_shape, flops, *args, far_in=(), scratch=()):
+    outs = jax.tree.leaves(out_shape)
+    args = [
+        pltpu.with_memory_space_constraint(x, pltpu.MemorySpace.HBM) if index in far_in else x
+        for index, x in enumerate(args)
+    ]
+    moved = sum(x.size * x.dtype.itemsize for x in (*args, *outs))
     return pl.pallas_call(
         kernel,
         out_shape=out_shape,
-        in_specs=[VMEM] * len(args),
+        in_specs=[HBM if index in far_in else VMEM for index in range(len(args))],
         out_specs=jax.tree.map(lambda _: VMEM, out_shape),
+        scratch_shapes=list(scratch),
         compiler_params=pltpu.CompilerParams(vmem_limit_bytes=16 * 1024 * 1024),
         cost_estimate=pl.CostEstimate(flops=flops, bytes_accessed=moved, transcendentals=0),
     )(*args)
 
 
-def marks_kernel(slot_ref, out_ref):
+def marks_kernel(far_slot_ref, far_length_ref, out_ref, share_ref, slot_ref, length_ref, arrived):
+    lengths = pltpu.make_async_copy(far_length_ref, length_ref, arrived.at[0])
+    slots = pltpu.make_async_copy(far_slot_ref, slot_ref, arrived.at[1])
+    lengths.start()
+    slots.start()
+    lengths.wait()
+    share_ref[...] = 1.0 / length_ref[...].astype(jnp.float32)
+    slots.wait()
     chips, cores, tables, _, samples = out_ref.shape
     for chip in range(chips):
         for core in range(cores):
@@ -77,11 +93,12 @@
                 out_ref[chip, :, start : start + samples] = total
 
 
-def other_half_kernel(scaled_ref, out_ref):
-    chips, tables = out_ref.shape[:2]
-    other = 1 - lax.axis_index("lane_1")
+def halves_kernel(scaled_ref, own_ref, other_ref):
+    chips, tables = own_ref.shape[:2]
+    core = lax.axis_index("lane_1")
     for chip in range(chips):
-        out_ref[chip] = scaled_ref[pl.ds((2 * chip + other) * tables, tables)]
+        own_ref[chip] = scaled_ref[pl.ds((2 * chip + core) * tables, tables)]
+        other_ref[chip] = scaled_ref[pl.ds((2 * chip + 1 - core) * tables, tables)]
 
 
 def products(counts_ref, chip, core, values):
@@ -94,13 +111,10 @@
     )
 
 
-def own_kernel(counts_ref, scaled_ref, out_ref):
+def own_kernel(counts_ref, values_ref, out_ref):
     core = lax.axis_index("lane_1")
-    chips = counts_ref.shape[0]
-    tables = scaled_ref.shape[0] // (2 * chips)
-    for chip in range(chips):
-        values = scaled_ref[pl.ds((2 * chip + core) * tables, tables)]
-        out_ref[chip] = products(counts_ref, chip, core, values)
+    for chip in range(counts_ref.shape[0]):
+        out_ref[chip] = products(counts_ref, chip, core, values_ref[chip])
 
 
 def pair_kernel(counts_ref, pair_ref, own_ref, out_ref):
@@ -132,18 +146,28 @@
     batch_rows, table_count, embed_width = grad_pooled.shape
     tables_here = table_count // lane_count
     bag_depth = lookup_slot.shape[2]
-    marks = kernel_call(
+    marks, share = kernel_call(
         marks_kernel,
-        jax.ShapeDtypeStruct((chips, cores, tables_here, bag_depth, batch_rows), jnp.bfloat16),
+        (
+            jax.ShapeDtypeStruct((chips, cores, tables_here, bag_depth, batch_rows), jnp.bfloat16),
+            jax.ShapeDtypeStruct((table_count, batch_rows), jnp.float32),
+        ),
         lookup_slot.size,
         lookup_slot.transpose(1, 2, 0),
+        bag_len.transpose(1, 0),
+        far_in=(0, 1),
+        scratch=(
+            pltpu.VMEM((tables_here, bag_depth, chips * cores * batch_rows), jnp.int32),
+            pltpu.VMEM((table_count, batch_rows), jnp.int32),
+            pltpu.SemaphoreType.DMA((2,)),
+        ),
     )
     marks = exchange(marks, "lane_0")
-    scaled = (grad_pooled.astype(jnp.float32) * (1.0 / bag_len.astype(jnp.float32))[:, :, None]).astype(jnp.bfloat16)
+    scaled = (grad_pooled.astype(jnp.float32) * share.transpose(1, 0)[:, :, None]).astype(jnp.bfloat16)
     scaled = scaled.transpose(1, 0, 2)
     half = jax.ShapeDtypeStruct((chips, tables_here, batch_rows, embed_width), jnp.bfloat16)
-    pair = kernel_call(other_half_kernel, half, half.size, scaled)
-    pair = lax.ppermute(pair, "lane_1", [(0, 1), (1, 0)])
+    values, other = kernel_call(halves_kernel, (half, half), 2 * half.size, scaled)
+    pair = lax.ppermute(other, "lane_1", [(0, 1), (1, 0)])
     terms = cores * tables_here * batch_rows
     counts = kernel_call(
         counts_kernel,
@@ -153,7 +177,7 @@
     )
     flops = chips * number_slots * terms * embed_width
     part_shape = (chips, number_slots, embed_width)
-    own = kernel_call(own_kernel, jax.ShapeDtypeStruct(part_shape, jnp.float32), flops, counts, scaled)
+    own = kernel_call(own_kernel, jax.ShapeDtypeStruct(part_shape, jnp.float32), flops, counts, values)
     own, targets = lax.optimization_barrier((own, slot_row.reshape(1, number_slots)))
     partial_value = kernel_call(pair_kernel, jax.ShapeDtypeStruct(part_shape, jnp.bfloat16), flops, counts, pair, own)
     partial_value = exchange(partial_value, "lane_0")

time: 94.3 us -> 93.4 us (level)
  transfers between devices with their start and end apart: 2 -> 2, of which waited for: 1 -> 1; matrix products, arithmetic and copies ran while one was open for 0% -> 0% of each run, Pallas kernels for 3% -> 2%
where the time goes in v5:
time: 93.4 us; the launch traced here: 92.9 us
  blocking collectives  63.6 us (68%)
  starting transfers between devices  15.7 us (17%)
  Pallas kernels  5.32 us (6%)
  waiting for transfers between devices  4.21 us (5%)
  other arithmetic  2.55 us (3%)
    all_to_all x4, blocking collectives, exchange(): return lax.all_to_all(x, axes, split_axis=0, concat_axis=0, tiled=True)  63.6 us
    ppermute x1, starting transfers between devices, per_device(): pair = lax.ppermute(other, 'lane_1', [(0, 1), (1, 0)])  12.4 us
    pallas_call x6, Pallas kernels, kernel_call(): pl.pallas_call(kernel, out_shape=out_shape, in_specs=[HBM if index in far...  5.32 us
    all_to_all x1, waiting for transfers between devices, exchange(): return lax.all_to_all(x, axes, split_axis=0, concat_axis=0, tiled=True)  4.2 us
    all_to_all x1, starting transfers between devices, exchange(): return lax.all_to_all(x, axes, split_axis=0, concat_axis=0, tiled=True)  3.3 us
    transpose x1, other arithmetic, per_device(): scaled = scaled.transpose(1, 0, 2)  2.45 us
  transfers between devices with their start and end apart: 2, of which 1 were waited for; matrix products, arithmetic and copies ran while one was open for 0% of the time, Pallas kernels for 2%

profile of v5, /device:TPU:1, one launch (start us, length us, event | category | flops | bytes accessed | tf_op | source)
XLA Modules:
  0.0 92.9 jit_solution(5624982924067172337)
XLA Ops:
  0.6 1.6 %shard_map.77 = (bf16[4,2,4,8,128]{4,3,2,1,0:T(8,128)(2,1)}, f32[32,128]{1,0:T(8,128)S(1)}) custom-call(s32[4,8,1024]{2,1,0:T(8,128)} %bitcast.15, s32[32,128]{1,0:T(8,128)} %bitcast.17), custom_call_target="tpu_custom_call" | custom-call | flops 32768 | bytes 229376 | tf_op jit(solution)/shard_map/pallas_call | solution.py:50
  2.2 2.4 %fusion.scaled_ref = bf16[32,128,256]{2,1,0:T(8,128)(2,1)S(1)} fusion(bf16[128,32,256]{2,1,0:T(8,128)(2,1)} %param.6, f32[128,32]{0,1:T(8,128)S(1)} %bitcast.14), kind=kLoop, calls=%fused_computation.1 | loop fusion | flops 3145728 | bytes 4210688 | tf_op jit(solution)/shard_map/transpose | solution.py:167
  4.7 0.0 copy-start.2
  4.7 0.1 shard_map.79
  4.8 12.4 %collective-permute-start = (bf16[4,4,128,256]{3,2,1,0:T(8,128)(2,1)S(1)}, bf16[4,4,128,256]{3,2,1,0:T(8,128)(2,1)S(1)}, u32[]{:S(2)}, u32[]{:S(2)}) collective-permute-start(bf16[4,4,128,256]{3,2,1,0:T(8,128)(2,1)S(1)} %get-tuple-element.14), channel_id=1, source_target_pairs={{0,1},{1,0},{2,3},{3,2},{4,5},{5,4},{6,7},{7,6},{8,9},{9,8},{10,11... | collective-permute-start | bytes 3145736 | tf_op jit(solution)/shard_map/ppermute | solution.py:170
  17.2 3.3 %all-to-all-start = ((bf16[4,2,4,8,128]{4,3,2,1,0:T(8,128)(2,1)}), bf16[4,2,4,8,128]{4,3,2,1,0:T(8,128)(2,1)S(1)}, u32[]{:S(2)}, u32[]{:S(2)}) async-start(bf16[4,2,4,8,128]{4,3,2,1,0:T(8,128)(2,1)} %get-tuple-element.10), calls=%async_computation | async-start | bytes 131072 | tf_op jit(solution)/shard_map/all_to_all | solution.py:24
  20.5 0.0 copy-done.2
  20.5 0.1 copy.14
  20.6 0.1 reshape.35
  20.8 4.2 %all-to-all-done.marks_ref = bf16[4,2,4,8,128]{4,3,2,1,0:T(8,128)(2,1)S(1)} async-done(((bf16[4,2,4,8,128]{4,3,2,1,0:T(8,128)(2,1)}), bf16[4,2,4,8,128]{4,3,2,1,0:T(8,128)(2,1)S(1)}, u32[]{:S(2)}, u32[]{:S(2)}) %all-to-all-start) | async-done | bytes 65568 | tf_op jit(solution)/shard_map/all_to_all | solution.py:24
  25.0 1.4 %shard_map.78.counts_ref = bf16[4,192,1024]{2,1,0:T(8,128)(2,1)S(1)} custom-call(bf16[4,2,4,8,128]{4,3,2,1,0:T(8,128)(2,1)S(1)} %all-to-all-done.marks_ref), custom_call_target="tpu_custom_call" | custom-call | flops 6291456 | bytes 1638400 | tf_op jit(solution)/shard_map/pallas_call | solution.py:50
  26.4 0.4 shard_map.80.own_ref
  26.7 0.0 collective-permute-done.pair_ref
  26.8 0.4 shard_map.81
  27.1 0.0 copy-start
  27.2 0.0 copy-start.1
  27.2 9.5 %all_to_all.25 = bf16[4,192,256]{2,1,0:T(8,128)(2,1)S(1)} all-to-all(bf16[4,192,256]{2,1,0:T(8,128)(2,1)S(1)} %shard_map.81), channel_id=1, replica_groups=mesh['grp_0'=12,'grp_1'=8,'lane_0'=4,'lane_1'=2] {'lane_0'}, dimensions={0} | all-to-all | bytes 786432 | tf_op jit(solution)/shard_map/all_to_all | solution.py:24
  36.7 0.1 reduce_sum.39
  36.8 26.2 %all_to_all.26 = bf16[96,2,256]{2,1,0:T(2,128)(2,1)S(1)} all-to-all(bf16[96,2,256]{2,1,0:T(2,128)(2,1)S(1)} %reshape.36), channel_id=1, replica_groups=mesh['grp_0'=12,'grp_1'=8,'lane_0'=4,'lane_1'=2] {'grp_0','grp_1'}, dimensions={0} | all-to-all | bytes 196608 | tf_op jit(solution)/shard_map/all_to_all | solution.py:24
  63.1 0.4 multiply_reduce_fusion
  63.6 16.1 %all_to_all.27 = f32[24,1,128]{2,1,0:T(1,128)S(1)} all-to-all(f32[24,1,128]{2,1,0:T(1,128)S(1)} %broadcast_in_dim.4), channel_id=1, replica_groups=mesh['grp_0'=12,'grp_1'=8,'lane_0'=4,'lane_1'=2] {'grp_0','lane_1'}, dimensions={0} | all-to-all | bytes 24576 | tf_op jit(solution)/shard_map/all_to_all | solution.py:24
  79.7 11.7 %all_to_all.28.norms_ref = f32[32,1,128]{2,1,0:T(1,128)S(1)} all-to-all(f32[32,1,128]{2,1,0:T(1,128)S(1)} %broadcast_in_dim.5), channel_id=1, replica_groups=mesh['grp_0'=12,'grp_1'=8,'lane_0'=4,'lane_1'=2] {'grp_1','lane_0'}, dimensions={0} | all-to-all | bytes 32768 | tf_op jit(solution)/shard_map/all_to_all | solution.py:24
  91.4 0.0 copy-done
  91.4 0.0 copy-done.1
  91.4 1.5 %shard_map.82 = (f32[4,256,256]{2,1,0:T(8,128)}, f32[4,256]{1,0:T(4,128)}) custom-call(f32[32,1,128]{2,1,0:T(1,128)S(1)} %all_to_all.28.norms_ref, f32[4,256]{1,0:T(4,128)S(1)} %div.13.square_ref, f32[4,256,256]{2,1,0:T(8,128)S(1)} %bitcast.13, f32[4,256,256]{2,1,0:T(8,128)S(1)} %copy-done, f32[4,256]{1,0:T(4,128)S(1)} %copy-done.1), custom_call_target="tpu_custom_call" | custom-call | flops 524288 | bytes 3174400 | tf_op jit(solution)/shard_map/pallas_call | solution.py:50
  (8 shorter events, 0.2 us)
Async XLA Ops:
  4.7 15.9 %copy-start.2 = (s32[1,1,96,2]{2,3,1,0:T(2,128)S(1)}, s32[1,1,96,2]{2,3,1,0:T(2,128)}, u32[]{:S(2)}) copy-start(s32[1,1,96,2]{2,3,1,0:T(2,128)} %param.9) | copy-start | bytes 2308
  4.8 21.9 %collective-permute-start = (bf16[4,4,128,256]{3,2,1,0:T(8,128)(2,1)S(1)}, bf16[4,4,128,256]{3,2,1,0:T(8,128)(2,1)S(1)}, u32[]{:S(2)}, u32[]{:S(2)}) collective-permute-start(bf16[4,4,128,256]{3,2,1,0:T(8,128)(2,1)S(1)} %get-tuple-element.14), channel_id=1, source_target_pairs={{0,1},{1,0},{2,3},{3,2},{4,5},{5,4},{6,7},{7,6},{8,9},{9,8},{10,11... | collective-permute-start | bytes 3145736 | tf_op jit(solution)/shard_map/ppermute | solution.py:170
  17.2 7.8 %all-to-all-start = ((bf16[4,2,4,8,128]{4,3,2,1,0:T(8,128)(2,1)}), bf16[4,2,4,8,128]{4,3,2,1,0:T(8,128)(2,1)S(1)}, u32[]{:S(2)}, u32[]{:S(2)}) async-start(bf16[4,2,4,8,128]{4,3,2,1,0:T(8,128)(2,1)} %get-tuple-element.10), calls=%async_computation | async-start | bytes 131072 | tf_op jit(solution)/shard_map/all_to_all | solution.py:24
  27.1 64.2 %copy-start = (f32[4,256,256]{2,1,0:T(8,128)S(1)}, f32[4,256,256]{2,1,0:T(8,128)}, u32[]{:S(2)}) copy-start(f32[4,256,256]{2,1,0:T(8,128)} %weights_ref.1) | copy-start | bytes 3145732
  27.2 64.2 %copy-start.1 = (f32[4,256]{1,0:T(4,128)S(1)}, f32[4,256]{1,0:T(4,128)}, u32[]{:S(2)}) copy-start(f32[4,256]{1,0:T(4,128)} %accum_ref.1) | copy-start | bytes 12292

commit v6 on v5

--- a/solution.py
+++ b/solution.py
@@ -3,6 +3,7 @@
 
 import jax
 import jax.numpy as jnp
+import numpy as np
 from jax import lax
 from jax.experimental import pallas as pl
 from jax.experimental.pallas import tpu as pltpu
@@ -16,6 +17,8 @@
 GRP_LANE = ("grp_0", "grp_1", "lane_0", "lane_1")
 
 
+FAR, FAR_Y = 10, 9
+
 LEARN_RATE = 0.3
 EPSILON = 1e-06
 
@@ -24,14 +27,29 @@
     return lax.all_to_all(x, axes, split_axis=0, concat_axis=0, tiled=True)
 
 
-def gathered(x, axes):
+def exchange_from(x, axes, begin):
     count = lax.axis_size(axes)
-    return exchange(jnp.broadcast_to(x.reshape(1, 1, 128), (count, 1, 128)), axes)
+    first = count * begin // 16
+    order = np.roll(np.arange(count), -first).tolist()
+    x = jnp.concatenate([x[first:], x[:first]], axis=0)
+    x = lax.all_to_all(x, axes, split_axis=0, concat_axis=0, tiled=True, axis_index_groups=[order])
+    return jnp.concatenate([x[count - first :], x[: count - first]], axis=0)
+
+
+def gathered(x, axes, begin):
+    sizes = [lax.axis_size(axis) for axis in GRP_LANE]
+    count = lax.axis_size(axes)
+    places = np.arange(math.prod(sizes)).reshape(sizes)
+    inner = [index for index, axis in enumerate(GRP_LANE) if axis in axes]
+    outer = [index for index, axis in enumerate(GRP_LANE) if axis not in axes]
+    groups = np.roll(places.transpose(outer + inner).reshape(-1, count), -(count * begin // 16), axis=1).tolist()
+    copies = jnp.broadcast_to(x.reshape(1, 1, 128), (count, 1, 128))
+    return lax.all_to_all(copies, GRP_LANE, split_axis=0, concat_axis=0, tiled=True, axis_index_groups=groups)
 
 
 def parts_of_sum(row):
-    row = jnp.sum(gathered(row, ("grp_0", "lane_1")), axis=0)
-    return gathered(row, ("grp_1", "lane_0"))
+    row = jnp.sum(gathered(row, ("grp_0", "lane_1"), FAR), axis=0)
+    return gathered(row, ("grp_1", "lane_0"), FAR_Y)
 
 
 VMEM = pl.BlockSpec(memory_space=pltpu.VMEM)
@@ -183,7 +201,7 @@
     partial_value = exchange(partial_value, "lane_0")
     slot_sum = jnp.sum(partial_value.astype(jnp.float32), axis=0).astype(jnp.bfloat16)
     outgoing = slot_sum.reshape(group_count, SLOTS_PEER, embed_width)
-    incoming = exchange(outgoing, GRP).reshape(number_slots, embed_width)
+    incoming = exchange_from(outgoing, GRP, FAR).reshape(number_slots, embed_width)
     local_rows = accum.shape[0] * accum.shape[1]
     row_ids = lax.broadcasted_iota(jnp.int32, (local_rows, 1), 0)
     placing = (row_ids == targets).astype(jnp.bfloat16)

time: 93.4 us -> 85.9 us (0.920)
  blocking collectives: 63.6 us -> 55.1 us
    all_to_all x4 -> x1, blocking collectives: 63.6 us -> 9.54 us  [exchange(): return lax.all_to_all(x, axes, split_axis=0, concat_axis=0, tiled=True)]
    all_to_all x0 -> x3, blocking collectives: none -> 45.6 us  [the longest x2 26.1 us: gathered(): lax.all_to_all(copies, GRP_LANE, split_axis=0, concat_axis=0, tiled=True,...]
where the time goes in v6:
time: 85.9 us; the launch traced here: 84.8 us
  blocking collectives  55.1 us (64%)
  starting transfers between devices  15.7 us (18%)
  Pallas kernels  5.32 us (6%)
  waiting for transfers between devices  4.21 us (5%)
  other arithmetic  2.81 us (3%)
    all_to_all x2, blocking collectives, gathered(): lax.all_to_all(copies, GRP_LANE, split_axis=0, concat_axis=0, tiled=True,...  26.1 us
    all_to_all x1, blocking collectives, exchange_from(): lax.all_to_all(x, axes, split_axis=0, concat_axis=0, tiled=True, axis_ind...  19.5 us
    ppermute x1, starting transfers between devices, per_device(): pair = lax.ppermute(other, 'lane_1', [(0, 1), (1, 0)])  12.4 us
    all_to_all x1, blocking collectives, exchange(): return lax.all_to_all(x, axes, split_axis=0, concat_axis=0, tiled=True)  9.54 us
    pallas_call x6, Pallas kernels, kernel_call(): pl.pallas_call(kernel, out_shape=out_shape, in_specs=[HBM if index in far...  5.32 us
    all_to_all x1, waiting for transfers between devices, exchange(): return lax.all_to_all(x, axes, split_axis=0, concat_axis=0, tiled=True)  4.2 us
    all_to_all x1, starting transfers between devices, exchange(): return lax.all_to_all(x, axes, split_axis=0, concat_axis=0, tiled=True)  3.3 us
    transpose x1, other arithmetic, per_device(): scaled = scaled.transpose(1, 0, 2)  2.45 us
  transfers between devices with their start and end apart: 2, of which 1 were waited for; matrix products, arithmetic and copies ran while one was open for 0% of the time, Pallas kernels for 2%

profile of v6, /device:TPU:1, one launch (start us, length us, event | category | flops | bytes accessed | tf_op | source)
XLA Modules:
  0.0 84.8 jit_solution(2495953282587276242)
XLA Ops:
  0.6 1.6 %shard_map.77 = (bf16[4,2,4,8,128]{4,3,2,1,0:T(8,128)(2,1)}, f32[32,128]{1,0:T(8,128)S(1)}) custom-call(s32[4,8,1024]{2,1,0:T(8,128)} %bitcast.15, s32[32,128]{1,0:T(8,128)} %bitcast.17), custom_call_target="tpu_custom_call" | custom-call | flops 32768 | bytes 229376 | tf_op jit(solution)/shard_map/pallas_call | solution.py:68
  2.2 2.4 %fusion.scaled_ref = bf16[32,128,256]{2,1,0:T(8,128)(2,1)S(1)} fusion(bf16[128,32,256]{2,1,0:T(8,128)(2,1)} %param.6, f32[128,32]{0,1:T(8,128)S(1)} %bitcast.14), kind=kLoop, calls=%fused_computation.1 | loop fusion | flops 3145728 | bytes 4210688 | tf_op jit(solution)/shard_map/transpose | solution.py:185
  4.7 0.0 copy-start.2
  4.7 0.1 shard_map.79
  4.8 12.4 %collective-permute-start = (bf16[4,4,128,256]{3,2,1,0:T(8,128)(2,1)S(1)}, bf16[4,4,128,256]{3,2,1,0:T(8,128)(2,1)S(1)}, u32[]{:S(2)}, u32[]{:S(2)}) collective-permute-start(bf16[4,4,128,256]{3,2,1,0:T(8,128)(2,1)S(1)} %get-tuple-element.14), channel_id=1, source_target_pairs={{0,1},{1,0},{2,3},{3,2},{4,5},{5,4},{6,7},{7,6},{8,9},{9,8},{10,11... | collective-permute-start | bytes 3145736 | tf_op jit(solution)/shard_map/ppermute | solution.py:188
  17.2 3.3 %all-to-all-start = ((bf16[4,2,4,8,128]{4,3,2,1,0:T(8,128)(2,1)}), bf16[4,2,4,8,128]{4,3,2,1,0:T(8,128)(2,1)S(1)}, u32[]{:S(2)}, u32[]{:S(2)}) async-start(bf16[4,2,4,8,128]{4,3,2,1,0:T(8,128)(2,1)} %get-tuple-element.10), calls=%async_computation | async-start | bytes 131072 | tf_op jit(solution)/shard_map/all_to_all | solution.py:27
  20.5 0.0 copy-done.2
  20.5 0.1 copy.14
  20.6 0.1 reshape.35
  20.8 4.2 %all-to-all-done.marks_ref = bf16[4,2,4,8,128]{4,3,2,1,0:T(8,128)(2,1)S(1)} async-done(((bf16[4,2,4,8,128]{4,3,2,1,0:T(8,128)(2,1)}), bf16[4,2,4,8,128]{4,3,2,1,0:T(8,128)(2,1)S(1)}, u32[]{:S(2)}, u32[]{:S(2)}) %all-to-all-start) | async-done | bytes 65568 | tf_op jit(solution)/shard_map/all_to_all | solution.py:27
  25.0 1.4 %shard_map.78.counts_ref = bf16[4,192,1024]{2,1,0:T(8,128)(2,1)S(1)} custom-call(bf16[4,2,4,8,128]{4,3,2,1,0:T(8,128)(2,1)S(1)} %all-to-all-done.marks_ref), custom_call_target="tpu_custom_call" | custom-call | flops 6291456 | bytes 1638400 | tf_op jit(solution)/shard_map/pallas_call | solution.py:68
  26.4 0.4 shard_map.80.own_ref
  26.7 0.0 collective-permute-done.pair_ref
  26.8 0.4 shard_map.81
  27.1 0.0 copy-start
  27.2 0.0 copy-start.1
  27.2 9.5 %all_to_all.25 = bf16[4,192,256]{2,1,0:T(8,128)(2,1)S(1)} all-to-all(bf16[4,192,256]{2,1,0:T(8,128)(2,1)S(1)} %shard_map.81), channel_id=1, replica_groups=mesh['grp_0'=12,'grp_1'=8,'lane_0'=4,'lane_1'=2] {'lane_0'}, dimensions={0} | all-to-all | bytes 786432 | tf_op jit(solution)/shard_map/all_to_all | solution.py:27
  36.7 0.1 reduce_sum.39
  36.9 0.1 pad_maximum_fusion
  37.0 19.5 %all_to_all.26 = bf16[96,2,256]{2,1,0:T(2,128)(2,1)S(1)} all-to-all(bf16[96,2,256]{2,1,0:T(2,128)(2,1)S(1)} %pad_maximum_fusion), channel_id=1, replica_groups={{480,488,496,504,512,520,528,536,544,552,560,568,576,584,592,600,608,61..., dimensions={0} | all-to-all | bytes 196608 | tf_op jit(solution)/shard_map/all_to_all | solution.py:35
  56.6 0.1 pad_maximum_fusion.1
  56.8 0.4 multiply_reduce_fusion
  57.2 15.5 %all_to_all.27 = f32[24,1,128]{2,1,0:T(1,128)S(1)} all-to-all(f32[24,1,128]{2,1,0:T(1,128)S(1)} %broadcast_in_dim.4), channel_id=1, replica_groups={{449,512,513,576,577,640,641,704,705,0,1,64,65,128,129,192,193,256,257,..., dimensions={0} | all-to-all | bytes 24576 | tf_op jit(solution)/shard_map/all_to_all | solution.py:47
  72.8 10.6 %all_to_all.28.norms_ref = f32[32,1,128]{2,1,0:T(1,128)S(1)} all-to-all(f32[32,1,128]{2,1,0:T(1,128)S(1)} %broadcast_in_dim.5), channel_id=1, replica_groups={{36,38,40,42,44,46,48,50,52,54,56,58,60,62,0,2,4,6,8,10,12,14,16,18,20,..., dimensions={0} | all-to-all | bytes 32768 | tf_op jit(solution)/shard_map/all_to_all | solution.py:47
  83.4 0.0 copy-done
  83.4 0.0 copy-done.1
  83.4 1.5 %shard_map.82 = (f32[4,256,256]{2,1,0:T(8,128)}, f32[4,256]{1,0:T(4,128)}) custom-call(f32[32,1,128]{2,1,0:T(1,128)S(1)} %all_to_all.28.norms_ref, f32[4,256]{1,0:T(4,128)S(1)} %div.13.square_ref, f32[4,256,256]{2,1,0:T(8,128)S(1)} %bitcast.13, f32[4,256,256]{2,1,0:T(8,128)S(1)} %copy-done, f32[4,256]{1,0:T(4,128)S(1)} %copy-done.1), custom_call_target="tpu_custom_call" | custom-call | flops 524288 | bytes 3174400 | tf_op jit(solution)/shard_map/pallas_call | solution.py:68
  (13 shorter events, 0.3 us)
Async XLA Ops:
  4.7 15.9 %copy-start.2 = (s32[1,1,96,2]{2,3,1,0:T(2,128)S(1)}, s32[1,1,96,2]{2,3,1,0:T(2,128)}, u32[]{:S(2)}) copy-start(s32[1,1,96,2]{2,3,1,0:T(2,128)} %param.9) | copy-start | bytes 2308
  4.8 21.9 %collective-permute-start = (bf16[4,4,128,256]{3,2,1,0:T(8,128)(2,1)S(1)}, bf16[4,4,128,256]{3,2,1,0:T(8,128)(2,1)S(1)}, u32[]{:S(2)}, u32[]{:S(2)}) collective-permute-start(bf16[4,4,128,256]{3,2,1,0:T(8,128)(2,1)S(1)} %get-tuple-element.14), channel_id=1, source_target_pairs={{0,1},{1,0},{2,3},{3,2},{4,5},{5,4},{6,7},{7,6},{8,9},{9,8},{10,11... | collective-permute-start | bytes 3145736 | tf_op jit(solution)/shard_map/ppermute | solution.py:188
  17.2 7.8 %all-to-all-start = ((bf16[4,2,4,8,128]{4,3,2,1,0:T(8,128)(2,1)}), bf16[4,2,4,8,128]{4,3,2,1,0:T(8,128)(2,1)S(1)}, u32[]{:S(2)}, u32[]{:S(2)}) async-start(bf16[4,2,4,8,128]{4,3,2,1,0:T(8,128)(2,1)} %get-tuple-element.10), calls=%async_computation | async-start | bytes 131072 | tf_op jit(solution)/shard_map/all_to_all | solution.py:27
  27.1 56.2 %copy-start = (f32[4,256,256]{2,1,0:T(8,128)S(1)}, f32[4,256,256]{2,1,0:T(8,128)}, u32[]{:S(2)}) copy-start(f32[4,256,256]{2,1,0:T(8,128)} %weights_ref.1) | copy-start | bytes 3145732
  27.2 56.2 %copy-start.1 = (f32[4,256]{1,0:T(4,128)S(1)}, f32[4,256]{1,0:T(4,128)}, u32[]{:S(2)}) copy-start(f32[4,256]{1,0:T(4,128)} %accum_ref.1) | copy-start | bytes 12292

commit v7 on v6

--- a/solution.py
+++ b/solution.py
@@ -17,14 +17,16 @@
 GRP_LANE = ("grp_0", "grp_1", "lane_0", "lane_1")
 
 
-FAR, FAR_Y = 10, 9
+FAR, FAR_Y, FAR_X = 10, 9, 2
 
 LEARN_RATE = 0.3
 EPSILON = 1e-06
 
 
-def exchange(x, axes):
-    return lax.all_to_all(x, axes, split_axis=0, concat_axis=0, tiled=True)
+def exchange_along_x(x):
+    chips = lax.axis_size("lane_0")
+    order = [(FAR_X + place) % chips for place in range(chips)]
+    return lax.all_to_all(x, "lane_0", split_axis=0, concat_axis=0, tiled=True, axis_index_groups=[order])
 
 
 def exchange_from(x, axes, begin):
@@ -89,7 +91,7 @@
         for core in range(cores):
             start = (chip * cores + core) * samples
             for table in range(tables):
-                out_ref[chip, core, table] = slot_ref[table, :, start : start + samples].astype(
+                out_ref[(chip - FAR_X) % chips, core, table] = slot_ref[table, :, start : start + samples].astype(
                     out_ref.dtype
                 )
 
@@ -104,7 +106,7 @@
             for table in range(tables):
                 total = None
                 for position in range(depth):
-                    mark = marks_ref[chip, core, table, position : position + 1, :]
+                    mark = marks_ref[(chip - FAR_X) % chips, core, table, position : position + 1, :]
                     hit = jnp.where(numbers == mark, one, zero)
                     total = hit if total is None else total + hit
                 start = (core * tables + table) * samples
@@ -137,9 +139,10 @@
 
 def pair_kernel(counts_ref, pair_ref, own_ref, out_ref):
     core = lax.axis_index("lane_1")
-    for chip in range(counts_ref.shape[0]):
+    chips = counts_ref.shape[0]
+    for chip in range(chips):
         both = own_ref[chip] + products(counts_ref, chip, 1 - core, pair_ref[chip])
-        out_ref[chip] = both.astype(out_ref.dtype)
+        out_ref[(chip - FAR_X) % chips] = both.astype(out_ref.dtype)
 
 
 def update_kernel(scale, limit, norms_ref, square_ref, rows_ref, weights_ref, accum_ref, new_weights_ref, new_accum_ref):
@@ -180,7 +183,7 @@
             pltpu.SemaphoreType.DMA((2,)),
         ),
     )
-    marks = exchange(marks, "lane_0")
+    marks = exchange_along_x(marks)
     scaled = (grad_pooled.astype(jnp.float32) * share.transpose(1, 0)[:, :, None]).astype(jnp.bfloat16)
     scaled = scaled.transpose(1, 0, 2)
     half = jax.ShapeDtypeStruct((chips, tables_here, batch_rows, embed_width), jnp.bfloat16)
@@ -198,7 +201,7 @@
     own = kernel_call(own_kernel, jax.ShapeDtypeStruct(part_shape, jnp.float32), flops, counts, values)
     own, targets = lax.optimization_barrier((own, slot_row.reshape(1, number_slots)))
     partial_value = kernel_call(pair_kernel, jax.ShapeDtypeStruct(part_shape, jnp.bfloat16), flops, counts, pair, own)
-    partial_value = exchange(partial_value, "lane_0")
+    partial_value = exchange_along_x(partial_value)
     slot_sum = jnp.sum(partial_value.astype(jnp.float32), axis=0).astype(jnp.bfloat16)
     outgoing = slot_sum.reshape(group_count, SLOTS_PEER, embed_width)
     incoming = exchange_from(outgoing, GRP, FAR).reshape(number_slots, embed_width)

time: 85.9 us -> 85.8 us (level)
  waiting for transfers between devices: 4.21 us -> 1.74 us
  blocking collectives: 55.1 us -> 56.9 us
  starting transfers between devices: 15.7 us -> 16.6 us
    all_to_all x1, waiting for transfers between devices: 4.2 us -> 1.74 us  [exchange_along_x(): lax.all_to_all(x, 'lane_0', split_axis=0, concat_axis=0, tiled=True, axis...]
    all_to_all x1, blocking collectives: 19.5 us -> 21.4 us  [exchange_from(): lax.all_to_all(x, axes, split_axis=0, concat_axis=0, tiled=True, axis_ind...]
    all_to_all x1, starting transfers between devices: 3.3 us -> 4.25 us  [exchange_along_x(): lax.all_to_all(x, 'lane_0', split_axis=0, concat_axis=0, tiled=True, axis...]
where the time goes in v7:
time: 85.8 us; the launch traced here: 85 us
  blocking collectives  56.9 us (66%)
  starting transfers between devices  16.6 us (19%)
  Pallas kernels  5.32 us (6%)
  other arithmetic  2.81 us (3%)
  waiting for transfers between devices  1.74 us (2%)
    all_to_all x2, blocking collectives, gathered(): lax.all_to_all(copies, GRP_LANE, split_axis=0, concat_axis=0, tiled=True,...  26.5 us
    all_to_all x1, blocking collectives, exchange_from(): lax.all_to_all(x, axes, split_axis=0, concat_axis=0, tiled=True, axis_ind...  21.4 us
    ppermute x1, starting transfers between devices, per_device(): pair = lax.ppermute(other, 'lane_1', [(0, 1), (1, 0)])  12.4 us
    all_to_all x1, blocking collectives, exchange_along_x(): lax.all_to_all(x, 'lane_0', split_axis=0, concat_axis=0, tiled=True, axis...  9.06 us
    pallas_call x6, Pallas kernels, kernel_call(): pl.pallas_call(kernel, out_shape=out_shape, in_specs=[HBM if index in far...  5.32 us
    all_to_all x1, starting transfers between devices, exchange_along_x(): lax.all_to_all(x, 'lane_0', split_axis=0, concat_axis=0, tiled=True, axis...  4.25 us
    transpose x1, other arithmetic, per_device(): scaled = scaled.transpose(1, 0, 2)  2.45 us
    all_to_all x1, waiting for transfers between devices, exchange_along_x(): lax.all_to_all(x, 'lane_0', split_axis=0, concat_axis=0, tiled=True, axis...  1.74 us
  transfers between devices with their start and end apart: 2, of which 1 were waited for; matrix products, arithmetic and copies ran while one was open for 0% of the time, Pallas kernels for 2%

profile of v7, /device:TPU:1, one launch (start us, length us, event | category | flops | bytes accessed | tf_op | source)
XLA Modules:
  0.0 85.0 jit_solution(18275965689876241635)
XLA Ops:
  0.6 1.6 %shard_map.77 = (bf16[4,2,4,8,128]{4,3,2,1,0:T(8,128)(2,1)}, f32[32,128]{1,0:T(8,128)S(1)}) custom-call(s32[4,8,1024]{2,1,0:T(8,128)} %bitcast.15, s32[32,128]{1,0:T(8,128)} %bitcast.17), custom_call_target="tpu_custom_call" | custom-call | flops 32768 | bytes 229376 | tf_op jit(solution)/shard_map/pallas_call | solution.py:70
  2.2 2.4 %fusion.scaled_ref = bf16[32,128,256]{2,1,0:T(8,128)(2,1)S(1)} fusion(bf16[128,32,256]{2,1,0:T(8,128)(2,1)} %param.6, f32[128,32]{0,1:T(8,128)S(1)} %bitcast.14), kind=kLoop, calls=%fused_computation.1 | loop fusion | flops 3145728 | bytes 4210688 | tf_op jit(solution)/shard_map/transpose | solution.py:188
  4.7 0.0 copy-start.2
  4.7 0.1 shard_map.79
  4.8 12.4 %collective-permute-start = (bf16[4,4,128,256]{3,2,1,0:T(8,128)(2,1)S(1)}, bf16[4,4,128,256]{3,2,1,0:T(8,128)(2,1)S(1)}, u32[]{:S(2)}, u32[]{:S(2)}) collective-permute-start(bf16[4,4,128,256]{3,2,1,0:T(8,128)(2,1)S(1)} %get-tuple-element.14), channel_id=1, source_target_pairs={{0,1},{1,0},{2,3},{3,2},{4,5},{5,4},{6,7},{7,6},{8,9},{9,8},{10,11... | collective-permute-start | bytes 3145736 | tf_op jit(solution)/shard_map/ppermute | solution.py:191
  17.2 4.2 %all-to-all-start = ((bf16[4,2,4,8,128]{4,3,2,1,0:T(8,128)(2,1)}), bf16[4,2,4,8,128]{4,3,2,1,0:T(8,128)(2,1)S(1)}, u32[]{:S(2)}, u32[]{:S(2)}) async-start(bf16[4,2,4,8,128]{4,3,2,1,0:T(8,128)(2,1)} %get-tuple-element.10), calls=%async_computation | async-start | bytes 131072 | tf_op jit(solution)/shard_map/all_to_all | solution.py:29
  21.5 0.0 copy-done.2
  21.5 0.1 copy.14
  21.6 0.1 reshape.35
  21.7 1.7 %all-to-all-done.marks_ref = bf16[4,2,4,8,128]{4,3,2,1,0:T(8,128)(2,1)S(1)} async-done(((bf16[4,2,4,8,128]{4,3,2,1,0:T(8,128)(2,1)}), bf16[4,2,4,8,128]{4,3,2,1,0:T(8,128)(2,1)S(1)}, u32[]{:S(2)}, u32[]{:S(2)}) %all-to-all-start) | async-done | bytes 65568 | tf_op jit(solution)/shard_map/all_to_all | solution.py:29
  23.5 1.4 %shard_map.78.counts_ref = bf16[4,192,1024]{2,1,0:T(8,128)(2,1)S(1)} custom-call(bf16[4,2,4,8,128]{4,3,2,1,0:T(8,128)(2,1)S(1)} %all-to-all-done.marks_ref), custom_call_target="tpu_custom_call" | custom-call | flops 6291456 | bytes 1638400 | tf_op jit(solution)/shard_map/pallas_call | solution.py:70
  24.8 0.4 shard_map.80.own_ref
  25.2 0.0 collective-permute-done.pair_ref
  25.2 0.4 shard_map.81
  25.6 0.0 copy-start
  25.6 0.0 copy-start.1
  25.6 9.1 %all_to_all.25 = bf16[4,192,256]{2,1,0:T(8,128)(2,1)S(1)} all-to-all(bf16[4,192,256]{2,1,0:T(8,128)(2,1)S(1)} %shard_map.81), channel_id=1, replica_groups={{4,6,0,2},{5,7,1,3},{12,14,8,10},{13,15,9,11},{20,22,16,18},{21,23,17,1..., dimensions={0} | all-to-all | bytes 786432 | tf_op jit(solution)/shard_map/all_to_all | solution.py:29
  34.7 0.1 reduce_sum.39
  34.8 0.1 pad_maximum_fusion
  35.0 21.4 %all_to_all.26 = bf16[96,2,256]{2,1,0:T(2,128)(2,1)S(1)} all-to-all(bf16[96,2,256]{2,1,0:T(2,128)(2,1)S(1)} %pad_maximum_fusion), channel_id=1, replica_groups={{480,488,496,504,512,520,528,536,544,552,560,568,576,584,592,600,608,61..., dimensions={0} | all-to-all | bytes 196608 | tf_op jit(solution)/shard_map/all_to_all | solution.py:37
  56.4 0.1 pad_maximum_fusion.1
  56.6 0.4 multiply_reduce_fusion
  57.1 15.0 %all_to_all.27 = f32[24,1,128]{2,1,0:T(1,128)S(1)} all-to-all(f32[24,1,128]{2,1,0:T(1,128)S(1)} %broadcast_in_dim.4), channel_id=1, replica_groups={{449,512,513,576,577,640,641,704,705,0,1,64,65,128,129,192,193,256,257,..., dimensions={0} | all-to-all | bytes 24576 | tf_op jit(solution)/shard_map/all_to_all | solution.py:49
  72.1 11.5 %all_to_all.28.norms_ref = f32[32,1,128]{2,1,0:T(1,128)S(1)} all-to-all(f32[32,1,128]{2,1,0:T(1,128)S(1)} %broadcast_in_dim.5), channel_id=1, replica_groups={{36,38,40,42,44,46,48,50,52,54,56,58,60,62,0,2,4,6,8,10,12,14,16,18,20,..., dimensions={0} | all-to-all | bytes 32768 | tf_op jit(solution)/shard_map/all_to_all | solution.py:49
  83.6 0.0 copy-done
  83.6 0.0 copy-done.1
  83.6 1.5 %shard_map.82 = (f32[4,256,256]{2,1,0:T(8,128)}, f32[4,256]{1,0:T(4,128)}) custom-call(f32[32,1,128]{2,1,0:T(1,128)S(1)} %all_to_all.28.norms_ref, f32[4,256]{1,0:T(4,128)S(1)} %div.13.square_ref, f32[4,256,256]{2,1,0:T(8,128)S(1)} %bitcast.13, f32[4,256,256]{2,1,0:T(8,128)S(1)} %copy-done, f32[4,256]{1,0:T(4,128)S(1)} %copy-done.1), custom_call_target="tpu_custom_call" | custom-call | flops 524288 | bytes 3174400 | tf_op jit(solution)/shard_map/pallas_call | solution.py:70
  (13 shorter events, 0.3 us)
Async XLA Ops:
  4.7 16.8 %copy-start.2 = (s32[1,1,96,2]{2,3,1,0:T(2,128)S(1)}, s32[1,1,96,2]{2,3,1,0:T(2,128)}, u32[]{:S(2)}) copy-start(s32[1,1,96,2]{2,3,1,0:T(2,128)} %param.9) | copy-start | bytes 2308
  4.8 20.4 %collective-permute-start = (bf16[4,4,128,256]{3,2,1,0:T(8,128)(2,1)S(1)}, bf16[4,4,128,256]{3,2,1,0:T(8,128)(2,1)S(1)}, u32[]{:S(2)}, u32[]{:S(2)}) collective-permute-start(bf16[4,4,128,256]{3,2,1,0:T(8,128)(2,1)S(1)} %get-tuple-element.14), channel_id=1, source_target_pairs={{0,1},{1,0},{2,3},{3,2},{4,5},{5,4},{6,7},{7,6},{8,9},{9,8},{10,11... | collective-permute-start | bytes 3145736 | tf_op jit(solution)/shard_map/ppermute | solution.py:191
  17.2 6.2 %all-to-all-start = ((bf16[4,2,4,8,128]{4,3,2,1,0:T(8,128)(2,1)}), bf16[4,2,4,8,128]{4,3,2,1,0:T(8,128)(2,1)S(1)}, u32[]{:S(2)}, u32[]{:S(2)}) async-start(bf16[4,2,4,8,128]{4,3,2,1,0:T(8,128)(2,1)} %get-tuple-element.10), calls=%async_computation | async-start | bytes 131072 | tf_op jit(solution)/shard_map/all_to_all | solution.py:29
  25.6 58.0 %copy-start = (f32[4,256,256]{2,1,0:T(8,128)S(1)}, f32[4,256,256]{2,1,0:T(8,128)}, u32[]{:S(2)}) copy-start(f32[4,256,256]{2,1,0:T(8,128)} %weights_ref.1) | copy-start | bytes 3145732
  25.6 57.9 %copy-start.1 = (f32[4,256]{1,0:T(4,128)S(1)}, f32[4,256]{1,0:T(4,128)}, u32[]{:S(2)}) copy-start(f32[4,256]{1,0:T(4,128)} %accum_ref.1) | copy-start | bytes 12292
